TPU v7x, 32 devices: a 4x4x1 block of a 4x4x8 slice. The times are simulated.
32 devices in a mesh: part: 1 (over z), tp: 4 (over y), dp: 8 (over x, core).
Axes of the slice: x: 4, y: 4, z: 1, core: 2. Of those that a mesh axis runs over, the one named last changes fastest.
The devices are a block of a 4x4x8 slice.
Arguments:
- hidden: bfloat16 [32, 2048, 2048], P(('part', 'dp', 'tp'))
- ln_gain: float32 [2048], replicated
- w_in: bfloat16 [2048, 18944], P(None, ('dp', 'tp'))
- w_out: bfloat16 [10240, 2048], P(('dp', 'tp'))
Outputs:
- output 1: bfloat16 [32, 2048, 2048], P(('part', 'dp', 'tp'))
- output 2: bfloat16 [32, 2048, 256], P(('part', 'dp', 'tp'))
- output 3: bfloat16 [32, 2048, 256], P(('part', 'dp', 'tp'))
All inputs are finite; a program needn't handle non-finite values.
Results may differ from a plain program's by a relative error of at most 0.00278234.
Values are sent between devices in bfloat16 or wider.
A program may use at most 768 MiB of HBM per device.

v0:
```python
import jax
import jax.numpy as jnp
from jax import lax
from jax.sharding import PartitionSpec as P

LN_EPS = 1e-6
ROPE_BASE = 10000.0
BLOCK_CAP = 512


def layer_norm(x_blk, ln_gain):
    x_wide = x_blk.astype(jnp.float32)
    centered = x_wide - jnp.mean(x_wide, axis=-1, keepdims=True)
    row_var = jnp.mean(centered * centered, axis=-1, keepdims=True)
    return (centered * lax.rsqrt(row_var + LN_EPS) * ln_gain).astype(jnp.bfloat16)


def rotary(values):
    seq_len = values.shape[1]
    head_dim = values.shape[-1]
    half_dim = head_dim // 2
    inv_freq = ROPE_BASE ** (-jnp.arange(half_dim, dtype=jnp.float32) * 2.0 / head_dim)
    angles = jnp.arange(seq_len, dtype=jnp.float32)[:, None] * inv_freq[None, :]
    tab_shape = (1, seq_len) + (1,) * (values.ndim - 3) + (half_dim,)
    cos_tab = jnp.cos(angles).reshape(tab_shape)
    sin_tab = jnp.sin(angles).reshape(tab_shape)
    first_half = values[..., :half_dim]
    second_half = values[..., half_dim:]
    return jnp.concatenate([first_half * cos_tab - second_half * sin_tab,
                            second_half * cos_tab + first_half * sin_tab], axis=-1)


def causal_mqa(q_rot, k_rot, v_all):
    n_batch, seq_len, n_heads, head_dim = q_rot.shape
    q_blk = min(seq_len, BLOCK_CAP)
    n_blk = seq_len // q_blk
    q_tiles = q_rot.reshape(n_batch, n_blk, q_blk, n_heads, head_dim)
    score_scale = head_dim ** -0.5
    key_pos = jnp.arange(seq_len)

    def one_block(blk_idx):
        q_tile = lax.dynamic_index_in_dim(q_tiles, blk_idx, axis=1, keepdims=False)
        scores = jnp.einsum('bqhe,bke->bqhk', q_tile, k_rot, preferred_element_type=jnp.float32) * score_scale
        q_pos = blk_idx * q_blk + jnp.arange(q_blk)
        allowed = key_pos[None, :] <= q_pos[:, None]
        scores = jnp.where(allowed[None, :, None, :], scores, -1e30)
        attn_prob = jax.nn.softmax(scores, axis=-1).astype(jnp.bfloat16)
        return jnp.einsum('bqhk,bke->bqhe', attn_prob, v_all, preferred_element_type=jnp.float32).astype(jnp.bfloat16)

    out_tiles = lax.map(one_block, jnp.arange(n_blk))
    return jnp.moveaxis(out_tiles, 0, 1).reshape(n_batch, seq_len, n_heads * head_dim)


def mix_rows(joint_rows, q_width, head_dim):
    n_batch, seq_len, joint_width = joint_rows.shape
    ff_width = (joint_width - q_width - 2 * head_dim) // 2
    gate_at = q_width + 2 * head_dim
    q_raw = joint_rows[..., :q_width].reshape(n_batch, seq_len, q_width // head_dim, head_dim)
    k_raw = joint_rows[..., q_width:q_width + head_dim]
    v_all = joint_rows[..., q_width + head_dim:gate_at]
    gate_proj = joint_rows[..., gate_at:gate_at + ff_width]
    up_proj = joint_rows[..., gate_at + ff_width:]
    q_rot = rotary(q_raw.astype(jnp.float32)).astype(jnp.bfloat16)
    k_rot = rotary(k_raw.astype(jnp.float32)).astype(jnp.bfloat16)
    attn_out = causal_mqa(q_rot, k_rot, v_all)
    mlp_out = (jax.nn.silu(gate_proj.astype(jnp.float32)) * up_proj.astype(jnp.float32)).astype(jnp.bfloat16)
    return jnp.concatenate([attn_out, mlp_out], axis=-1), k_rot, v_all


def solution(mesh):
    tok_spec = P(('part', 'dp', 'tp'))

    def per_device(x_blk, ln_gain, w_in_blk, w_out_blk):
        w_in = lax.all_gather(w_in_blk, ('dp', 'tp'), axis=1, tiled=True)
        w_out = lax.all_gather(w_out_blk, ('dp', 'tp'), axis=0, tiled=True)
        ff_width = 4 * x_blk.shape[-1]
        q_width = w_out.shape[0] - ff_width
        head_dim = (w_in.shape[1] - w_out.shape[0] - ff_width) // 2
        h_rows = layer_norm(x_blk, ln_gain)
        joint_rows = jnp.einsum('bsd,dc->bsc', h_rows, w_in, preferred_element_type=jnp.float32).astype(jnp.bfloat16)
        mixed_rows, k_rot, v_all = mix_rows(joint_rows, q_width, head_dim)
        proj_out = jnp.einsum('bsz,zd->bsd', mixed_rows, w_out, preferred_element_type=jnp.float32)
        y_blk = (x_blk.astype(jnp.float32) + proj_out).astype(jnp.bfloat16)
        return y_blk, k_rot, v_all

    return jax.shard_map(per_device, mesh=mesh,
                         in_specs=(tok_spec, P(), P(None, ('dp', 'tp')), P(('dp', 'tp'), None)),
                         out_specs=(tok_spec, tok_spec, tok_spec), check_vma=False)
```

profile of v0, /device:TPU:97, one launch (start us, length us, event | category | flops | bytes accessed | tf_op | source)
XLA Modules:
  0.0 799.1 jit_solution(17539684720788745545)
XLA Ops:
  7.2 0.0 copy-start.2
  7.2 0.1 all-gather.3.cloned.1.call-start
  7.3 0.7 all-gather.3.cloned.1.call-update
  8.0 0.1 all-gather.5.cloned.1.call-start
  8.1 0.7 all-gather.5.cloned.1.call-update
  8.8 0.0 slice-start
  8.8 0.0 copy-start.3
  8.8 4.7 convert_reduce_fusion
  13.5 0.0 slice-start.1
  13.6 5.8 fusion.41
  19.4 0.0 copy-done.3
  19.4 4.9 fusion.53
  24.4 0.0 copy-done.2
  24.4 0.0 slice-done
  24.4 0.0 slice-done.1
  24.4 5.1 fusion.67
  29.4 208.2 %all-gather.3.cloned.1.call-done = bf16[2048,18944]{0,1:T(8,128)(2,1)} async-done(((bf16[2048,592]{0,1:T(8,128)(2,1)}), bf16[2048,18944]{0,1:T(8,128)(2,1)}) %all-gather.3.cloned.1.call-update) | async-done | bytes 77594640 | tf_op jit(solution)/shard_map/all_gather | solution.py:74
  237.6 175.0 %convert_bitcast_fusion.1 = bf16[1,2048,18944]{2,1,0:T(8,128)(2,1)} fusion(bf16[2048,18944]{0,1:T(8,128)(2,1)} %all-gather.3.cloned.1.call-done, bf16[2048,2048]{1,0:T(8,128)(2,1)} %fusion.67), kind=kOutput, calls=%fused_computation.29 | convolution fusion | flops 158952587264 | bytes 163577856 | tf_op jit(solution)/shard_map/bsd,dc->bsc/dot_general | solution.py:80
  412.6 11.4 %slice_convert_fusion = f32[1,2048,2048]{2,1,0:T(8,128)} fusion(bf16[1,2048,18944]{2,1,0:T(8,128)(2,1)} %convert_bitcast_fusion.1), kind=kLoop, calls=%fused_computation.49 | loop fusion | flops 4194304 | bytes 25165824 | tf_op jit(solution)/shard_map/convert_element_type | solution.py:63
  424.0 0.0 copy-start.4
  424.0 0.0 copy-start
  424.0 0.0 copy-start.1
  424.0 15.9 %copy.13 = f32[256,8,8,256]{3,2,1,0:T(8,128)} copy(f32[256,8,8,256]{3,1,2,0:T(8,128)} %bitcast.94) | data formatting | bytes 33554432
  439.8 2.7 fusion.60
  442.6 0.0 copy-done.4
  442.6 4.3 subtract_convert_fusion.1
  446.9 1.1 pad_maximum_fusion.1
  448.0 0.0 copy-done
  448.0 0.0 copy-done.1
  448.0 8.8 %subtract_convert_fusion = (bf16[1,2048,8,128]{3,2,1,0:T(8,128)(2,1)S(1)}, bf16[1,2048,8,128]{3,2,1,0:T(8,128)(2,1)}) fusion(f32[1,2048,8,256]{3,2,1,0:T(8,128)} %bitcast.95, f32[2048,128]{1,0:T(8,128)S(1)} %copy-done.1, f32[2048,128]{1,0:T(8,128)S(1)} %copy-done), kind=kLoop, calls=%fused_computation.52 | loop fusion | flops 16777216 | bytes 27262976 | tf_op jit(solution)/shard_map/convert.6
  456.8 6.5 pad_maximum_fusion
  463.3 182.4 %while.11 = (s32[]{:T(128)}, bf16[4,1,512,8,256]{4,3,2,0,1:T(8,128)(2,1)}, s32[4]{0:T(128)S(1)}, bf16[1,4,512,8,256]{4,3,2,1,0:T(8,128)(2,1)}, bf16[1,2048,256]{...) while((s32[]{:T(128)}, ...), condition=%wide.region_5.6_spmd.clone, body=%wide.region_2.5_spmd.clone.sunk | while | flops 12962504704 | bytes 21009064 | solution.py:50
  463.5 0.7 dynamic_slice.14
  466.0 1.7 constant_dynamic-slice_fusion.2
  468.3 0.7 iota_compare_fusion.2
  469.0 13.3 %fusion.76 = f32[512,8]{0,1:T(8,128)S(1)} fusion(pred[512,2048]{1,0:T(8,128)(4,1)S(1)} %iota_compare_fusion.2, bf16[1,1,512,8,256]{4,3,2,1,0:T(8,128)(2,1)S(1)} %constant_dynamic-slice_fusion.2, bf16[1,2048,256]{2,1,0:T(8,128)(2,1)} %get-tuple-element.142), kind=kOutput, calls=%fused_computation.70.clone.1 | convolution fusion | flops 4328523776 | bytes 4210688 | tf_op jit(solution)/shard_map/while/body/eval_jaxpr/sub | solution.py:47
  482.3 22.6 %convert_bitcast_fusion.3 = bf16[1,1,512,8,256]{4,2,3,1,0:T(8,128)(2,1)} fusion(f32[512,8]{0,1:T(8,128)S(1)} %fusion.76, bf16[1,2048,256]{2,1,0:T(8,128)(2,1)} %get-tuple-element.143, pred[512,2048]{1,0:T(8,128)(4,1)S(1)} %iota_compare_fusion.2, bf16[1,1,512,8,256]{4,3,2,1,0:T(8,128)(2,1)S(1)} %constant_dynamic-slice_fusion.2, ...), kind=kOutput, calls=%fused_computation.14.clone.1 | convolution fusion | flops 8632932352 | bytes 7356416 | tf_op jit(solution)/shard_map/while/body/eval_jaxpr/bqhk,bke->bqhe/dot_general | solution.py:48
  504.9 4.1 copy_dynamic-update-slice_fusion.2
  509.0 0.6 dynamic_slice.14
  511.5 1.7 constant_dynamic-slice_fusion.2
  513.9 0.7 iota_compare_fusion.2
  514.5 13.3 %fusion.76 = f32[512,8]{0,1:T(8,128)S(1)} fusion(pred[512,2048]{1,0:T(8,128)(4,1)S(1)} %iota_compare_fusion.2, bf16[1,1,512,8,256]{4,3,2,1,0:T(8,128)(2,1)S(1)} %constant_dynamic-slice_fusion.2, bf16[1,2048,256]{2,1,0:T(8,128)(2,1)} %get-tuple-element.142), kind=kOutput, calls=%fused_computation.70.clone.1 | convolution fusion | flops 4328523776 | bytes 4210688 | tf_op jit(solution)/shard_map/while/body/eval_jaxpr/sub | solution.py:47
  527.8 22.6 %convert_bitcast_fusion.3 = bf16[1,1,512,8,256]{4,2,3,1,0:T(8,128)(2,1)} fusion(f32[512,8]{0,1:T(8,128)S(1)} %fusion.76, bf16[1,2048,256]{2,1,0:T(8,128)(2,1)} %get-tuple-element.143, pred[512,2048]{1,0:T(8,128)(4,1)S(1)} %iota_compare_fusion.2, bf16[1,1,512,8,256]{4,3,2,1,0:T(8,128)(2,1)S(1)} %constant_dynamic-slice_fusion.2, ...), kind=kOutput, calls=%fused_computation.14.clone.1 | convolution fusion | flops 8632932352 | bytes 7356416 | tf_op jit(solution)/shard_map/while/body/eval_jaxpr/bqhk,bke->bqhe/dot_general | solution.py:48
  550.4 4.1 copy_dynamic-update-slice_fusion.2
  554.5 0.6 dynamic_slice.14
  557.0 1.7 constant_dynamic-slice_fusion.2
  559.4 0.7 iota_compare_fusion.2
  560.0 13.3 %fusion.76 = f32[512,8]{0,1:T(8,128)S(1)} fusion(pred[512,2048]{1,0:T(8,128)(4,1)S(1)} %iota_compare_fusion.2, bf16[1,1,512,8,256]{4,3,2,1,0:T(8,128)(2,1)S(1)} %constant_dynamic-slice_fusion.2, bf16[1,2048,256]{2,1,0:T(8,128)(2,1)} %get-tuple-element.142), kind=kOutput, calls=%fused_computation.70.clone.1 | convolution fusion | flops 4328523776 | bytes 4210688 | tf_op jit(solution)/shard_map/while/body/eval_jaxpr/sub | solution.py:47
  573.3 22.6 %convert_bitcast_fusion.3 = bf16[1,1,512,8,256]{4,2,3,1,0:T(8,128)(2,1)} fusion(f32[512,8]{0,1:T(8,128)S(1)} %fusion.76, bf16[1,2048,256]{2,1,0:T(8,128)(2,1)} %get-tuple-element.143, pred[512,2048]{1,0:T(8,128)(4,1)S(1)} %iota_compare_fusion.2, bf16[1,1,512,8,256]{4,3,2,1,0:T(8,128)(2,1)S(1)} %constant_dynamic-slice_fusion.2, ...), kind=kOutput, calls=%fused_computation.14.clone.1 | convolution fusion | flops 8632932352 | bytes 7356416 | tf_op jit(solution)/shard_map/while/body/eval_jaxpr/bqhk,bke->bqhe/dot_general | solution.py:48
  595.9 4.1 copy_dynamic-update-slice_fusion.2
  600.0 0.6 dynamic_slice.14
  602.5 1.7 constant_dynamic-slice_fusion.2
  604.9 0.7 iota_compare_fusion.2
  605.5 13.3 %fusion.76 = f32[512,8]{0,1:T(8,128)S(1)} fusion(pred[512,2048]{1,0:T(8,128)(4,1)S(1)} %iota_compare_fusion.2, bf16[1,1,512,8,256]{4,3,2,1,0:T(8,128)(2,1)S(1)} %constant_dynamic-slice_fusion.2, bf16[1,2048,256]{2,1,0:T(8,128)(2,1)} %get-tuple-element.142), kind=kOutput, calls=%fused_computation.70.clone.1 | convolution fusion | flops 4328523776 | bytes 4210688 | tf_op jit(solution)/shard_map/while/body/eval_jaxpr/sub | solution.py:47
  618.8 22.6 %convert_bitcast_fusion.3 = bf16[1,1,512,8,256]{4,2,3,1,0:T(8,128)(2,1)} fusion(f32[512,8]{0,1:T(8,128)S(1)} %fusion.76, bf16[1,2048,256]{2,1,0:T(8,128)(2,1)} %get-tuple-element.143, pred[512,2048]{1,0:T(8,128)(4,1)S(1)} %iota_compare_fusion.2, bf16[1,1,512,8,256]{4,3,2,1,0:T(8,128)(2,1)S(1)} %constant_dynamic-slice_fusion.2, ...), kind=kOutput, calls=%fused_computation.14.clone.1 | convolution fusion | flops 8632932352 | bytes 7356416 | tf_op jit(solution)/shard_map/while/body/eval_jaxpr/bqhk,bke->bqhe/dot_general | solution.py:48
  641.4 4.1 copy_dynamic-update-slice_fusion.2
  645.7 13.4 %reshape_transpose.3 = bf16[1,2048,2048]{2,1,0:T(8,128)(2,1)} reshape(bf16[4,1,512,8,256]{4,3,2,0,1:T(8,128)(2,1)} %get-tuple-element.40) | data formatting | bytes 16777216 | tf_op jit(solution)/shard_map/reshape;transpose | solution.py:51
  659.2 33.5 %fusion.35 = bf16[1,2048,8192]{2,1,0:T(8,128)(2,1)} fusion(bf16[1,2048,18944]{2,1,0:T(8,128)(2,1)} %convert_bitcast_fusion.1), kind=kLoop, calls=%fused_computation.34 | loop fusion | flops 134217728 | bytes 100663296 | tf_op jit(solution)/shard_map/convert_element_type | solution.py:66
  692.7 0.0 all-gather.5.cloned.1.call-done
  692.7 99.4 %fusion.44 = bf16[1,2048,2048]{2,1,0:T(8,128)(2,1)} fusion(bf16[1,2048,2048]{2,1,0:T(8,128)(2,1)} %param.6, bf16[10240,2048]{1,0:T(8,128)(2,1)} %all-gather.5.cloned.1.call-done, bf16[1,2048,8192]{2,1,0:T(8,128)(2,1)} %fusion.35, bf16[1,2048,2048]{2,1,0:T(8,128)(2,1)} %reshape_transpose.3), kind=kOutput, calls=%fused_computation.47 | convolution fusion | flops 85995814912 | bytes 100663296 | tf_op jit(solution)/shard_map/bsz,zd->bsd/dot_general | solution.py:82
  (10 shorter events, 0.0 us)
Async XLA Ops:
  7.2 17.2 %copy-start.2 = (f32[2048]{0:T(1024)S(1)}, f32[2048]{0:T(1024)}, u32[]{:S(2)}) copy-start(f32[2048]{0:T(1024)} %param.7) | copy-start | bytes 24580
  7.2 230.4 %all-gather.3.cloned.1.call-start = ((), (), s32[]{:S(2)}) async-start(), calls=%async_computation | async-start | bytes 80019456 | tf_op jit(solution)/shard_map/all_gather | solution.py:74
  8.0 684.7 %all-gather.5.cloned.1.call-start = ((), (), s32[]{:S(2)}) async-start(), calls=%async_computation.1 | async-start | bytes 43253760 | tf_op jit(solution)/shard_map/all_gather | solution.py:75
  8.8 15.6 %slice-start = ((s8[8388608]{0:T(1024)(128)(4,1)}), s8[4194304]{0:T(1024)(128)(4,1)S(1)}, s32[]{:S(2)}) async-start(s8[8388608]{0:T(1024)(128)(4,1)} %bitcast.92), calls=%async_computation.2 | async-start | bytes 8388608
  8.8 10.6 %copy-start.3 = (f32[128]{0:T(128)}, f32[128]{0:T(128)S(1)}, u32[]{:S(2)}) copy-start(f32[128]{0:T(128)S(1)} %multiply_power_fusion) | copy-start | bytes 1540
  13.5 10.8 %slice-start.1 = ((s8[8388608]{0:T(1024)(128)(4,1)}), s8[4194304]{0:T(1024)(128)(4,1)S(1)}, s32[]{:S(2)}) async-start(s8[8388608]{0:T(1024)(128)(4,1)} %bitcast.92), calls=%async_computation.3 | async-start | bytes 8388608
  424.0 18.6 %copy-start.4 = (f32[128]{0:T(128)S(1)}, f32[128]{0:T(128)}, u32[]{:S(2)}) copy-start(f32[128]{0:T(128)} %copy-done.3) | copy-start | bytes 1540
  424.0 24.0 %copy-start = (f32[2048,128]{1,0:T(8,128)S(1)}, f32[2048,128]{1,0:T(8,128)}, u32[]{:S(2)}) copy-start(f32[2048,128]{1,0:T(8,128)} %get-tuple-element.79) | copy-start | bytes 3145732
  424.0 24.0 %copy-start.1 = (f32[2048,128]{1,0:T(8,128)S(1)}, f32[2048,128]{1,0:T(8,128)}, u32[]{:S(2)}) copy-start(f32[2048,128]{1,0:T(8,128)} %get-tuple-element.80) | copy-start | bytes 3145732
Sparse Core Ops, SparseCore 0:
  10.1 227.4 all-gather.2
  239.7 129.3 all-gather.4
where the time goes:
time: 804 us; the launch traced here: 799 us
  matrix products  418 us (52%)
  waiting for transfers between devices  210 us (26%)
  other arithmetic  91.5 us (11%)
  local copies, waits for them, and re-layouts  55.2 us (7%)
  between operations  14.4 us (2%)
  loops' own time  10.4 us (1%)
    all_gather x1, waiting for transfers between devices, per_device(): w_in = lax.all_gather(w_in_blk, ('dp', 'tp'), axis=1, tiled=True)  208 us
    dot_general x1, matrix products, per_device(): jnp.einsum('bsd,dc->bsc', h_rows, w_in, preferred_element_type=jnp.float32)  175 us
    dot_general x1, matrix products, per_device(): jnp.einsum('bsz,zd->bsd', mixed_rows, w_out, preferred_element_type=jnp.f...  99.4 us
    dot_general x4, matrix products, one_block(): jnp.einsum('bqhk,bke->bqhe', attn_prob, v_all, preferred_element_type=jnp...  90.4 us
    sub x4, matrix products, one_block(): attn_prob = jax.nn.softmax(scores, axis=-1).astype(jnp.bfloat16)  53.1 us
    convert_element_type x1, other arithmetic, mix_rows(): (jax.nn.silu(gate_proj.astype(jnp.float32)) * up_proj.astype(jnp.float32)...  33.5 us
    dynamic_update_slice x4, local copies, waits for them, and re-layouts, causal_mqa(): out_tiles = lax.map(one_block, jnp.arange(n_blk))  16.4 us
  transfers between devices with their start and end apart: 2, of which 1 were waited for; matrix products, arithmetic and copies ran while one was open for 58% of the time, Pallas kernels for 0%

commit v1 on v0

v1 whole, which is shorter than its diff:
```python
import functools

import jax
import jax.numpy as jnp
from jax import lax
from jax.experimental import pallas as pl
from jax.experimental.pallas import tpu as pltpu
from jax.sharding import PartitionSpec as P

LN_EPS = 1e-6
ROPE_BASE = 10000.0


def layer_norm(x, ln_gain):
    x_wide = x.astype(jnp.float32)
    centered = x_wide - jnp.mean(x_wide, axis=-1, keepdims=True)
    row_var = jnp.mean(centered * centered, axis=-1, keepdims=True)
    return (centered * lax.rsqrt(row_var + LN_EPS) * ln_gain).astype(jnp.bfloat16)


def rope_tables(seq_len, head_dim):
    half = head_dim // 2
    inv_freq = ROPE_BASE ** (-jnp.arange(half, dtype=jnp.float32) * 2.0 / head_dim)
    angles = jnp.arange(seq_len, dtype=jnp.float32)[:, None] * inv_freq[None, :]
    return jnp.cos(angles), jnp.sin(angles)


def attention_call(rows, k_arr, v_arr, cos_tab, sin_tab, n_heads, head_dim, fresh_k):
    seq_len = rows.shape[0]
    half = head_dim // 2
    tq, kstep, pair = 256, 512, 2
    n_q, n_len = seq_len // tq, seq_len // kstep
    scale = (head_dim ** -0.5) * 1.4426950408889634

    def rope(a, cos, sin):
        a = a.astype(jnp.float32)
        lo, hi = a[:, :half], a[:, half:]
        return jnp.concatenate([lo * cos - hi * sin, hi * cos + lo * sin], axis=1).astype(jnp.bfloat16)

    def body(q_ref, k_ref, v_ref, cos_ref, sin_ref, o_ref, *caches):
        qi, hp = pl.program_id(0), pl.program_id(1)
        ks_ref, vs_ref = caches if fresh_k else (k_ref, v_ref)

        if fresh_k:
            @pl.when(jnp.logical_and(qi == 0, hp == 0))
            def _():
                def one(j, c):
                    r = pl.ds(pl.multiple_of(j * kstep, kstep), kstep)
                    ks_ref[r, :] = rope(k_ref[r, :], cos_ref[r, :], sin_ref[r, :])
                    vs_ref[r, :] = v_ref[r, :]
                    return c
                lax.fori_loop(0, n_len, one, 0)

        trow = pl.ds(pl.multiple_of(qi * tq, tq), tq)
        cos, sin = cos_ref[trow, :], sin_ref[trow, :]

        def span(length):
            keys = ks_ref[0:length, :]
            vals = vs_ref[0:length, :]
            k_pos = (length - kstep) + lax.broadcasted_iota(jnp.int32, (tq, kstep), 1)
            q_pos = qi * tq + lax.broadcasted_iota(jnp.int32, (tq, kstep), 0)
            allowed = k_pos <= q_pos
            for j in range(pair):
                cols = slice(j * head_dim, (j + 1) * head_dim)
                q = rope(q_ref[:, cols], cos, sin)
                s = lax.dot_general(q, keys, (((1,), (1,)), ((), ())), preferred_element_type=jnp.float32) * scale
                last = jnp.where(allowed, s[:, length - kstep:], -1e30)
                s = jnp.concatenate([s[:, :length - kstep], last], axis=1) if length > kstep else last
                top = jnp.max(s, axis=1, keepdims=True)
                e = jnp.exp2(s - top)
                tot = jnp.sum(e, axis=1, keepdims=True)
                pr = (e * (1.0 / tot)).astype(jnp.bfloat16)
                o_ref[:, cols] = jnp.dot(pr, vals, preferred_element_type=jnp.float32).astype(jnp.bfloat16)

        for b in range(n_len):
            pl.when(qi // (kstep // tq) == b)(functools.partial(span, (b + 1) * kstep))

    whole = pl.BlockSpec((seq_len, head_dim), lambda i, h: (0, 0))
    tab = pl.BlockSpec((seq_len, half), lambda i, h: (0, 0))
    out_specs = [pl.BlockSpec((tq, pair * head_dim), lambda i, h: (i, h))]
    out_shape = [jax.ShapeDtypeStruct((seq_len, n_heads * head_dim), jnp.bfloat16)]
    if fresh_k:
        k_arr = v_arr = rows
        kv_specs = [pl.BlockSpec((seq_len, head_dim), lambda i, h: (0, n_heads)),
                    pl.BlockSpec((seq_len, head_dim), lambda i, h: (0, n_heads + 1))]
        out_specs += [whole, whole]
        out_shape += [jax.ShapeDtypeStruct((seq_len, head_dim), jnp.bfloat16)] * 2
    else:
        kv_specs = [whole, whole]
    flops = 4 * n_heads * seq_len * seq_len * head_dim * 5 // 8
    return pl.pallas_call(
        body,
        grid=(n_q, n_heads // pair),
        in_specs=[pl.BlockSpec((tq, pair * head_dim), lambda i, h: (i, h))] + kv_specs + [tab, tab],
        out_specs=out_specs,
        out_shape=out_shape,
        compiler_params=pltpu.CompilerParams(dimension_semantics=("arbitrary", "arbitrary"),
                                             vmem_limit_bytes=40 * 1024 * 1024),
        cost_estimate=pl.CostEstimate(flops=flops, bytes_accessed=16 * 1024 * 1024, transcendentals=0),
        name="mqa_a" if fresh_k else "mqa_b",
    )(rows, k_arr, v_arr, cos_tab, sin_tab)


def in_proj_call(chunk, h_t, p_t, dep, first, n_dev, block, offset, name):
    rows = chunk.shape[0] // n_dev
    depth, n_tok = h_t.shape
    n_grp = n_dev - first
    g = next(c for c in (7, 4, 2, 1) if n_grp % c == 0)
    steps = n_grp // g
    m = g * rows
    tn = min(512, n_tok)
    n_in = 2 + (p_t is not None) + (dep is not None)

    def body(*refs):
        chunk_ref, h_ref = refs[0], refs[1]
        out_ref, lbuf, obuf, lsem, osem = refs[n_in:]

        def load(s):
            return pltpu.make_async_copy(chunk_ref.at[pl.ds(first * rows + s * m, m), :], lbuf.at[s % 2], lsem.at[s % 2])

        def stores(s):
            return [pltpu.make_async_copy(obuf.at[s % 2, pl.ds(i * rows, rows), :],
                                          out_ref.at[pl.ds((s * g + i) * block + offset, rows), :],
                                          osem.at[s % 2, i]) for i in range(g)]

        load(0).start()
        for s in range(steps):
            if s + 1 < steps:
                load(s + 1).start()
            load(s).wait()
            if s >= 2:
                for c in stores(s - 2):
                    c.wait()

            def tile(n, carry):
                cols = pl.ds(pl.multiple_of(n * tn, tn), tn)
                obuf[s % 2, :, cols] = jnp.dot(lbuf[s % 2], h_ref[:, cols],
                                               preferred_element_type=jnp.float32).astype(jnp.bfloat16)
                return carry
            lax.fori_loop(0, n_tok // tn, tile, 0)
            for c in stores(s):
                c.start()
        for s in range(max(0, steps - 2), steps):
            for c in stores(s):
                c.wait()

    any_spec = pl.BlockSpec(memory_space=pl.ANY)
    args, specs, alias = [chunk, h_t], [any_spec, pl.BlockSpec(memory_space=pltpu.VMEM)], {}
    if p_t is not None:
        alias = {len(args): 0}
        args.append(p_t)
        specs.append(any_spec)
    if dep is not None:
        args.append(dep)
        specs.append(any_spec)
    total = n_grp * block
    return pl.pallas_call(
        body,
        in_specs=specs,
        out_specs=any_spec,
        out_shape=jax.ShapeDtypeStruct((total, n_tok), jnp.bfloat16),
        input_output_aliases=alias,
        scratch_shapes=[pltpu.VMEM((2, m, depth), jnp.bfloat16), pltpu.VMEM((2, m, n_tok), jnp.bfloat16),
                        pltpu.SemaphoreType.DMA((2,)), pltpu.SemaphoreType.DMA((2, g))],
        compiler_params=pltpu.CompilerParams(vmem_limit_bytes=48 * 1024 * 1024),
        cost_estimate=pl.CostEstimate(flops=2 * n_grp * rows * depth * n_tok,
                                      bytes_accessed=2 * n_grp * rows * (depth + n_tok), transcendentals=0),
        name=name,
    )(*args)


PIECE = 64


def out_proj_call(p_t, w_chunk, at, per, per_dev, q_width, gate_at, ff, acc, last):
    n_tok, d_out = p_t.shape[1], w_chunk.shape[1]
    n_all = w_chunk.shape[0] // PIECE
    q_pieces = q_width // PIECE
    full, tail = 8, 4
    first = sum(1 for z in range(q_pieces) if at <= z % per_dev < at + per)
    count = n_all - first
    steps, rest = divmod(count, full)
    assert rest in (0, tail)
    kk = full * PIECE
    tt = min(512, n_tok)
    n_t = n_tok // tt

    def body(*refs):
        if last is None:
            p_ref, w_ref, out_ref, acc_ref, gbuf, ubuf, wbuf, sem = refs
        else:
            (p_ref, w_ref, accin_ref, w0_ref, a0_ref, a1_ref, x_ref, out_ref,
             acc_ref, gbuf, ubuf, wbuf, sem, abuf, xbuf, asem, xsem, osem) = refs

        def copies(s, slot, n):
            row = pl.multiple_of((first + s * full) * PIECE, PIECE) if not isinstance(s, int) else (first + s * full) * PIECE
            res = [pltpu.make_async_copy(w_ref.at[pl.ds(row, n * PIECE), :],
                                         wbuf.at[slot, pl.ds(0, n * PIECE), :], sem.at[slot, 0])]
            for j in range(n):
                o = first + s * full + j
                dst = pl.ds(j * PIECE, PIECE)
                if isinstance(s, int):
                    row = gate_at + (per_dev * (o // per) + at + o % per - q_pieces) * PIECE
                else:
                    z = per_dev * lax.div(o, per) + at + lax.rem(o, per) - q_pieces
                    row = pl.multiple_of(gate_at + z * PIECE, PIECE)
                res.append(pltpu.make_async_copy(p_ref.at[pl.ds(row, PIECE), :], gbuf.at[slot, dst, :],
                                                 sem.at[slot, 1 + j]))
                res.append(pltpu.make_async_copy(p_ref.at[pl.ds(row + ff, PIECE), :], ubuf.at[slot, dst, :],
                                                 sem.at[slot, 1 + full + j]))
            return res

        def start(s, slot, n):
            for c in copies(s, slot, n):
                c.start()

        def finish(s, slot, n):
            for c in copies(s, slot, n):
                c.wait()

        def mlp(slot, n, fresh):
            k = n * PIECE
            for t in range(n_t):
                tok = slice(t * tt, (t + 1) * tt)
                g = gbuf[slot, 0:k, tok].astype(jnp.float32)
                u = ubuf[slot, 0:k, tok].astype(jnp.float32)
                m = (g * (1.0 / (1.0 + jnp.exp(-g))) * u).astype(jnp.bfloat16)
                prod = lax.dot_general(m, wbuf[slot, 0:k, :], (((0,), (0,)), ((), ())), preferred_element_type=jnp.float32)
                if fresh:
                    acc_ref[tok, :] = prod
                else:
                    acc_ref[tok, :] += prod

        start(0, 0, full)
        if last is not None:
            acc_in = pltpu.make_async_copy(accin_ref, acc_ref, xsem.at[0])
            acc_in.start()
            x_in = pltpu.make_async_copy(x_ref, xbuf, xsem.at[1])
            x_in.start()
            acc_in.wait()
        else:
            start(1, 1, full)
            finish(0, 0, full)
            mlp(0, full, True)
        lo = 0 if last is not None else 1

        def step(s, carry):
            slot = lax.rem(s, 2)

            @pl.when(s + 1 < steps)
            def _():
                start(s + 1, 1 - slot, full)
            if rest:
                @pl.when(s + 1 == steps)
                def _():
                    start(steps, 1 - slot, tail)
            finish(s, slot, full)
            mlp(slot, full, False)
            return carry

        lax.fori_loop(lo, steps, step, 0)
        if last is not None:
            heads = a0_ref.shape[1] // kk
            srcs = [(a0_ref, i, 0) for i in range(heads)] + [(a1_ref, i, 1) for i in range(heads)]

            def attn_copies(i):
                ref, blk, odd = srcs[i]
                slot = i % 2
                res = [pltpu.make_async_copy(ref.at[:, pl.ds(blk * kk, kk)], abuf.at[slot], asem.at[slot, 0])]
                for j in range(full):
                    half, r = divmod(j, full // 2)
                    head = 2 * (2 * blk + half) + odd
                    z = head * (full // 2) + r
                    dev, loc = divmod(z, per_dev)
                    if loc < at:
                        src = w0_ref.at[pl.ds((dev * at + loc) * PIECE, PIECE), :]
                    else:
                        src = w_ref.at[pl.ds((dev * per + loc - at) * PIECE, PIECE), :]
                    res.append(pltpu.make_async_copy(src, wbuf.at[slot, pl.ds(j * PIECE, PIECE), :], asem.at[slot, 1 + j]))
                return res

        if rest:
            finish(steps, steps % 2, tail)
            mlp(steps % 2, tail, False)

        if last is None:
            out = pltpu.make_async_copy(acc_ref, out_ref, sem.at[0, 0])
            out.start()
            out.wait()
        else:
            for c in attn_copies(0):
                c.start()
            for i in range(len(srcs)):
                if i + 1 < len(srcs):
                    for c in attn_copies(i + 1):
                        c.start()
                for c in attn_copies(i):
                    c.wait()
                for t in range(n_t):
                    tok = slice(t * tt, (t + 1) * tt)
                    acc_ref[tok, :] += jnp.dot(abuf[i % 2, tok, :], wbuf[i % 2], preferred_element_type=jnp.float32)
            x_in.wait()
            outs = []
            for t in range(n_t):
                tok = slice(t * tt, (t + 1) * tt)
                xbuf[tok, :] = (xbuf[tok, :].astype(jnp.float32) + acc_ref[tok, :]).astype(jnp.bfloat16)
                c = pltpu.make_async_copy(xbuf.at[pl.ds(t * tt, tt), :], out_ref.at[pl.ds(t * tt, tt), :], osem.at[t])
                c.start()
                outs.append(c)
            for c in outs:
                c.wait()

    any_spec = pl.BlockSpec(memory_space=pl.ANY)
    args = [p_t, w_chunk]
    scratch = [pltpu.VMEM((n_tok, d_out), jnp.float32)] + [pltpu.VMEM((2, kk, n_tok), jnp.bfloat16)] * 2
    scratch += [pltpu.VMEM((2, kk, d_out), jnp.bfloat16), pltpu.SemaphoreType.DMA((2, 1 + 2 * full))]
    out_dtype = jnp.float32
    if last is not None:
        w_first, a0, a1, x = last
        args += [acc, w_first, a0, a1, x]
        scratch += [pltpu.VMEM((2, n_tok, kk), jnp.bfloat16), pltpu.VMEM((n_tok, d_out), jnp.bfloat16),
                    pltpu.SemaphoreType.DMA((2, 1 + full)), pltpu.SemaphoreType.DMA((2,)), pltpu.SemaphoreType.DMA((n_t,))]
        out_dtype = jnp.bfloat16
    k_total = count * PIECE + (q_width if last is not None else 0)
    return pl.pallas_call(
        body,
        in_specs=[any_spec] * len(args),
        out_specs=any_spec,
        out_shape=jax.ShapeDtypeStruct((n_tok, d_out), out_dtype),
        scratch_shapes=scratch,
        compiler_params=pltpu.CompilerParams(vmem_limit_bytes=60 * 1024 * 1024),
        cost_estimate=pl.CostEstimate(flops=2 * k_total * n_tok * d_out, bytes_accessed=6 * k_total * d_out, transcendentals=0),
        name="out_proj_b" if last is not None else "out_proj_a",
    )(*args)


UNIT = 16
EARLY_UNITS = (5, 8, 8)
LATE_UNITS = (11, 5)
FIRST_PIECES = 3


def solution(mesh):
    tok_spec = P(('part', 'dp', 'tp'))
    group = ('dp', 'tp')
    n_dev = mesh.shape['dp'] * mesh.shape['tp']

    def per_device(x_blk, ln_gain, w_in_blk, w_out_blk):
        x = x_blk[0]
        seq_len, d_model = x.shape
        ff = 4 * d_model
        block = w_in_blk.shape[1]
        out_block = w_out_blk.shape[0]
        q_width = out_block * n_dev - ff
        head_dim = (block * n_dev - q_width - 2 * ff) // 2
        n_heads = q_width // head_dim
        n_qkv = q_width + 2 * head_dim
        first = n_qkv // block
        gate_at = n_qkv - first * block
        early_rows = block - head_dim
        cuts = [(2 * d + 1) * head_dim - d * block for d in range(first)]
        assert 2 * first == n_heads and all(0 <= c <= early_rows for c in cuts)
        assert sum(EARLY_UNITS) * UNIT == early_rows and sum(LATE_UNITS) * UNIT == head_dim
        w_rows = w_in_blk.T
        me = lax.axis_index('dp') * mesh.shape['tp'] + lax.axis_index('tp')
        cut = jnp.where(me < first, head_dim - (block - 2 * head_dim) * me, early_rows)
        below = lax.broadcasted_iota(jnp.int32, (early_rows, 1), 0) < cut
        early_local = jnp.where(below, w_rows[:early_rows], w_rows[head_dim:])
        late_local = lax.dynamic_slice_in_dim(w_rows, cut, head_dim, axis=0)

        chunks, offset = [], 0
        for local, units in ((early_local, EARLY_UNITS), (late_local, LATE_UNITS)):
            at = 0
            for u in units:
                chunks.append((lax.all_gather(local[at:at + u * UNIT], group, axis=0, tiled=True), offset))
                at += u * UNIT
                offset += u * UNIT
        cut_out = FIRST_PIECES * PIECE
        w_out_a = lax.all_gather(w_out_blk[:cut_out], group, axis=0, tiled=True)
        w_out_b = lax.all_gather(w_out_blk[cut_out:], group, axis=0, tiled=True)

        h = layer_norm(x, ln_gain)
        h_t = h.T
        cos_tab, sin_tab = rope_tables(seq_len, head_dim)

        def head_rows(parts):
            return jnp.concatenate([c.reshape(n_dev, -1, d_model) for c, _ in parts], axis=1)

        def project(w):
            return lax.dot_general(h, w, (((1,), (1,)), ((), ())), preferred_element_type=jnp.float32).astype(jnp.bfloat16)

        n_early = len(EARLY_UNITS)
        p_t = None
        for i, (c, off) in enumerate(chunks[:n_early]):
            p_t = in_proj_call(c, h_t, p_t, None, first, n_dev, block, off, f"in_proj_{i}")
        tops = [c.reshape(n_dev, -1, d_model)[:first] for c, _ in chunks[:n_early]]
        rest, left = [], gate_at
        for c, _ in chunks[:n_early]:
            per = c.shape[0] // n_dev
            take = min(left, per)
            if take:
                rest.append(c[first * per:first * per + take])
            left -= take
        w_a = jnp.concatenate([jnp.concatenate(tops, axis=1).reshape(-1, d_model)] + rest, axis=0)
        attn_a, k_rot, v_all = attention_call(project(w_a), None, None, cos_tab, sin_tab, n_heads // 2, head_dim, True)
        dep = attn_a
        for i, (c, off) in enumerate(chunks[n_early:]):
            p_t = in_proj_call(c, h_t, p_t, dep, first, n_dev, block, off, f"in_proj_{n_early + i}")
            dep = None
        tops = [c.reshape(n_dev, -1, d_model)[:first] for c, _ in chunks[n_early:]]
        w_b = jnp.concatenate(tops, axis=1).reshape(-1, d_model)
        attn_b = attention_call(project(w_b), k_rot, v_all, cos_tab, sin_tab, n_heads // 2, head_dim, False)[0]

        per_dev = out_block // PIECE
        acc = out_proj_call(p_t, w_out_a, 0, FIRST_PIECES, per_dev, q_width, gate_at, ff, None, None)
        y = out_proj_call(p_t, w_out_b, FIRST_PIECES, per_dev - FIRST_PIECES, per_dev, q_width, gate_at, ff, acc,
                          (w_out_a, attn_a, attn_b, x))
        return y[None], k_rot[None], v_all[None]

    return jax.shard_map(per_device, mesh=mesh,
                         in_specs=(tok_spec, P(), P(None, group), P(group, None)),
                         out_specs=(tok_spec, tok_spec, tok_spec), check_vma=False)
```

time: 804 us -> 664 us (0.83)
  matrix products: 418 us -> 31.3 us
  Pallas kernels: 0 us -> 377 us
  other arithmetic: 91.5 us -> 27.4 us
  waiting for transfers between devices: 210 us -> 175 us
  local copies, waits for them, and re-layouts: 55.2 us -> 32.8 us
  loops' own time: 10.4 us -> 0 us
    pallas_call x0 -> x9, Pallas kernels: none -> 377 us  [the longest x5 194 us: in_proj_call(): pl.pallas_call(body, in_specs=specs, out_specs=any_spec, out_shape=jax.Sh...]
    dot_general x6 -> x2, matrix products: 365 us -> 31.3 us  [project(): lax.dot_general(h, w, (((1,), (1,)), ((), ())), preferred_element_type=jn...]
    sub x4 -> x0, matrix products: 53.1 us -> none  [one_block(): attn_prob = jax.nn.softmax(scores, axis=-1).astype(jnp.bfloat16)]
    convert_element_type x2 -> x0, other arithmetic: 44.9 us -> none  [the longest x1 33.5 us: mix_rows(): (jax.nn.silu(gate_proj.astype(jnp.float32)) * up_proj.astype(jnp.float32)...]
    all_gather x2 -> x7, waiting for transfers between devices: 208 us -> 174 us  [the longest x5 174 us: per_device(): lax.all_gather(local[at:at + u * UNIT], group, axis=0, tiled=True)]
    slice x0 -> x16, local copies, waits for them, and re-layouts: none -> 16.9 us  [the longest x3 7.47 us: per_device(): tops = [c.reshape(n_dev, -1, d_model)[:first] for c, _ in chunks[:n_early]]]
    dynamic_update_slice x4 -> x0, local copies, waits for them, and re-layouts: 16.4 us -> none  [causal_mqa(): out_tiles = lax.map(one_block, jnp.arange(n_blk))]
    another operation x1 -> x0, local copies, waits for them, and re-layouts: 13.4 us -> none  [causal_mqa(): jnp.moveaxis(out_tiles, 0, 1).reshape(n_batch, seq_len, n_heads * head_dim)]
  transfers between devices with their start and end apart: 2 -> 7, of which waited for: 1 -> 4; matrix products, arithmetic and copies ran while one was open for 58% -> 13% of each run, Pallas kernels for 0% -> 47%
where the time goes in v1:
time: 664 us; the launch traced here: 659 us
  Pallas kernels  377 us (57%)
  waiting for transfers between devices  175 us (26%)
  local copies, waits for them, and re-layouts  32.8 us (5%)
  matrix products  31.3 us (5%)
  other arithmetic  27.4 us (4%)
  between operations  14.8 us (2%)
    pallas_call x5, Pallas kernels, in_proj_call(): pl.pallas_call(body, in_specs=specs, out_specs=any_spec, out_shape=jax.Sh...  194 us
    all_gather x5, waiting for transfers between devices, per_device(): lax.all_gather(local[at:at + u * UNIT], group, axis=0, tiled=True)  174 us
    pallas_call x2, Pallas kernels, out_proj_call(): pl.pallas_call(body, in_specs=[any_spec] * len(args), out_specs=any_spec,...  123 us
    pallas_call x2, Pallas kernels, attention_call(): pl.pallas_call(body, grid=(n_q, n_heads // pair), in_specs=[pl.BlockSpec(...  60 us
    dot_general x2, matrix products, project(): lax.dot_general(h, w, (((1,), (1,)), ((), ())), preferred_element_type=jn...  31.3 us
  transfers between devices with their start and end apart: 7, of which 4 were waited for; matrix products, arithmetic and copies ran while one was open for 13% of the time, Pallas kernels for 47%

profile of v1, /device:TPU:97, one launch (start us, length us, event | category | flops | bytes accessed | tf_op | source)
XLA Modules:
  0.0 658.7 jit_solution(522422937284753630)
XLA Ops:
  7.2 0.1 all-gather.16.cloned.1.call-start
  7.3 2.0 slice_select_fusion
  9.2 0.7 slice.90
  10.0 0.1 all-gather.16.cloned.1.call-update
  10.0 0.1 all-gather.8.cloned.1.call-start
  10.1 1.3 dynamic-slice_bitcast_fusion
  11.4 0.8 slice.84
  12.2 0.1 all-gather.8.cloned.1.call-update
  12.2 0.1 all-gather.14.cloned.1.call-start
  12.3 1.0 fusion.24
  13.3 0.1 all-gather.14.cloned.1.call-update
  13.4 0.1 all-gather.12.cloned.1.call-start
  13.5 0.6 all-gather.12.cloned.1.call-update
  14.0 0.1 all-gather.10.cloned.1.call-start
  14.1 0.9 slice.85
  15.0 0.1 all-gather.10.cloned.1.call-update
  15.1 0.1 all-gather.20.cloned.1.call-start
  15.2 2.1 slice.79
  17.3 0.1 all-gather.20.cloned.1.call-update
  17.3 0.1 all-gather.18.cloned.1.call-start
  17.4 1.9 slice.78
  19.3 0.1 all-gather.18.cloned.1.call-update
  19.4 0.0 slice-start
  19.4 0.0 copy-start.6
  19.4 4.7 convert_reduce_fusion
  24.1 0.0 slice-start.1
  24.1 5.8 fusion.2
  30.0 0.0 slice-done
  30.0 0.0 copy-done.6
  30.0 0.0 slice-done.1
  30.0 5.3 fusion.23
  35.3 11.8 %copy.15.refs_1_ = bf16[2048,2048]{1,0:T(8,128)(2,1)} copy(bf16[2048,2048]{0,1:T(8,128)(2,1)} %fusion.23) | data formatting | bytes 16777216 | tf_op jit(solution)/shard_map/transpose | solution.py:383
  47.1 3.9 fusion.19
  51.0 15.7 %all-gather.16.cloned.1.call-done.refs_0_ = bf16[2560,2048]{1,0:T(8,128)(2,1)} async-done(((bf16[80,2048]{1,0:T(8,128)(2,1)}), bf16[2560,2048]{1,0:T(8,128)(2,1)}) %all-gather.16.cloned.1.call-update) | async-done | bytes 10485776 | tf_op jit(solution)/shard_map/all_gather | solution.py:375
  66.7 2.6 slice.91
  69.3 51.3 %all-gather.8.cloned.1.call-done.refs_0_ = bf16[2560,2048]{1,0:T(8,128)(2,1)} async-done(((bf16[80,2048]{1,0:T(8,128)(2,1)}), bf16[2560,2048]{1,0:T(8,128)(2,1)}) %all-gather.8.cloned.1.call-update) | async-done | bytes 10485776 | tf_op jit(solution)/shard_map/all_gather | solution.py:375
  120.6 28.4 %in_proj_0.1.refs_2_ = bf16[16576,2048]{1,0:T(8,128)(2,1)} custom-call(bf16[2560,2048]{1,0:T(8,128)(2,1)} %all-gather.16.cloned.1.call-done.refs_0_, bf16[2048,2048]{1,0:T(8,128)(2,1)} %copy.15.refs_1_), custom_call_target="tpu_custom_call" | custom-call | flops 18790481920 | bytes 18350080 | tf_op jit(solution)/shard_map/in_proj_0/pallas_call | solution.py:157
  149.0 41.1 %all-gather.14.cloned.1.call-done.refs_0_ = bf16[4096,2048]{1,0:T(8,128)(2,1)} async-done(((bf16[128,2048]{1,0:T(8,128)(2,1)}), bf16[4096,2048]{1,0:T(8,128)(2,1)}) %all-gather.14.cloned.1.call-update) | async-done | bytes 16777232 | tf_op jit(solution)/shard_map/all_gather | solution.py:375
  190.0 3.2 slice.92
  193.2 66.1 %all-gather.12.cloned.1.call-done.refs_0_ = bf16[4096,2048]{1,0:T(8,128)(2,1)} async-done(((bf16[128,2048]{1,0:T(8,128)(2,1)}), bf16[4096,2048]{1,0:T(8,128)(2,1)}) %all-gather.12.cloned.1.call-update) | async-done | bytes 16777232 | tf_op jit(solution)/shard_map/all_gather | solution.py:375
  259.3 1.7 slice.93
  261.0 5.2 pad_maximum_fusion
  266.2 0.0 slice-done.2
  266.2 0.0 slice-done.3
  266.2 19.4 %convolution_convert_fusion.q_ref.k_ref.v_ref = bf16[2048,1536]{1,0:T(8,128)(2,1)} fusion(bf16[112,2048]{1,0:T(8,128)(2,1)S(1)} %slice-done.2, bf16[80,2048]{1,0:T(8,128)(2,1)S(1)} %slice-done.3, bf16[1344,2048]{1,0:T(8,128)(2,1)} %bitcast.38, f32[2048]{0:T(1024)S(1)} %copy-done.6, f32[2048]{0:T(1024)S(1)} %add_rsqrt_fusion, ...), kind=kOutput, calls=%fused_computation.13 | convolution fusion | flops 12927893504 | bytes 20996096 | tf_op jit(solution)/shard_map/dot_general | solution.py:390
  285.6 2.8 copy-done.5
  288.4 30.8 %mqa_a.1 = (bf16[2048,1024]{1,0:T(8,128)(2,1)S(1)}, bf16[2048,256]{1,0:T(8,128)(2,1)}, bf16[2048,256]{1,0:T(8,128)(2,1)}) custom-call(bf16[2048,1536]{1,0:T(8,128)(2,1)S(1)} %copy-done.5, bf16[2048,1536]{1,0:T(8,128)(2,1)S(1)} %copy-done.5, bf16[2048,1536]{1,0:T(8,128)(2,1)S(1)} %copy-done.5, f32[2048,128]{1,0:T(8,128)S(1)} %get-tuple-element.12.cos_ref, ...), custom_call_target="tpu_custom_call" | custom-call | flops 10737418240 | bytes 16777216 | tf_op jit(solution)/shard_map/mqa_a/pallas_call | solution.py:91
  319.3 42.1 %in_proj_1.1.refs_2_ = bf16[16576,2048]{1,0:T(8,128)(2,1)} custom-call(bf16[4096,2048]{1,0:T(8,128)(2,1)} %all-gather.14.cloned.1.call-done.refs_0_, bf16[2048,2048]{1,0:T(8,128)(2,1)} %copy.15.refs_1_, bf16[16576,2048]{1,0:T(8,128)(2,1)} %in_proj_0.1.refs_2_), custom_call_target="tpu_custom_call", output_to_operand_aliasing={{}: (2, {})} | custom-call | flops 30064771072 | bytes 29360128 | tf_op jit(solution)/shard_map/in_proj_1/pallas_call | solution.py:157
  361.4 0.0 copy-done
  361.4 0.0 slice-start.4
  361.4 40.6 %in_proj_2.1.refs_2_ = bf16[16576,2048]{1,0:T(8,128)(2,1)} custom-call(bf16[4096,2048]{1,0:T(8,128)(2,1)} %all-gather.12.cloned.1.call-done.refs_0_, bf16[2048,2048]{1,0:T(8,128)(2,1)} %copy.15.refs_1_, bf16[16576,2048]{1,0:T(8,128)(2,1)} %in_proj_1.1.refs_2_), custom_call_target="tpu_custom_call", output_to_operand_aliasing={{}: (2, {})} | custom-call | flops 30064771072 | bytes 29360128 | tf_op jit(solution)/shard_map/in_proj_2/pallas_call | solution.py:157
  402.0 0.0 all-gather.10.cloned.1.call-done.refs_0_
  402.0 2.0 slice.96
  404.0 0.5 pad_maximum_fusion.1
  404.5 0.0 copy-start.2
  404.6 0.0 copy-start.3
  404.6 11.9 %fusion.16.q_ref = bf16[2048,1024]{1,0:T(8,128)(2,1)S(1)} fusion(bf16[1024,2048]{1,0:T(8,128)(2,1)S(1)} %bitcast.40, bf16[1,2048,2048]{2,1,0:T(8,128)(2,1)} %param.4, f32[2048]{0:T(1024)S(1)} %copy-done.6, f32[2048]{0:T(1024)S(1)} %add_rsqrt_fusion, f32[2048]{0:T(1024)S(1)} %broadcast_multiply_fusion), kind=kOutput, calls=%fused_computation.21 | convolution fusion | flops 8613003264 | bytes 16801792 | tf_op jit(solution)/shard_map/dot_general | solution.py:390
  416.5 29.1 %mqa_b.1.refs_5_ = bf16[2048,1024]{1,0:T(8,128)(2,1)S(1)} custom-call(bf16[2048,1024]{1,0:T(8,128)(2,1)S(1)} %fusion.16.q_ref, bf16[2048,256]{1,0:T(8,128)(2,1)S(1)} %copy-done.2, bf16[2048,256]{1,0:T(8,128)(2,1)S(1)} %copy-done.3, f32[2048,128]{1,0:T(8,128)S(1)} %get-tuple-element.12.cos_ref, f32[2048,128]{1,0:T(8,128)S(1)} %get-tuple-element.11.sin_ref), custom_call_target="tpu_custom_call" | custom-call | flops 10737418240 | bytes 16777216 | tf_op jit(solution)/shard_map/mqa_b/pallas_call | solution.py:91
  445.6 54.9 %in_proj_3.1.refs_2_ = bf16[16576,2048]{1,0:T(8,128)(2,1)} custom-call(bf16[5632,2048]{1,0:T(8,128)(2,1)} %all-gather.10.cloned.1.call-done.refs_0_, bf16[2048,2048]{1,0:T(8,128)(2,1)} %copy.15.refs_1_, bf16[16576,2048]{1,0:T(8,128)(2,1)} %in_proj_2.1.refs_2_, bf16[2048,1024]{1,0:T(8,128)(2,1)S(1)} %copy-done.1), custom_call_target="tpu_custom_call", output_to_operand_aliasing={{}: (2, {})} | custom-call | flops 41339060224 | bytes 40370176 | tf_op jit(solution)/shard_map/in_proj_3/pallas_call | solution.py:157
  500.5 28.4 %in_proj_4.1.refs_0_ = bf16[16576,2048]{1,0:T(8,128)(2,1)} custom-call(bf16[2560,2048]{1,0:T(8,128)(2,1)} %all-gather.8.cloned.1.call-done.refs_0_, bf16[2048,2048]{1,0:T(8,128)(2,1)} %copy.15.refs_1_, bf16[16576,2048]{1,0:T(8,128)(2,1)} %in_proj_3.1.refs_2_), custom_call_target="tpu_custom_call", output_to_operand_aliasing={{}: (2, {})} | custom-call | flops 18790481920 | bytes 18350080 | tf_op jit(solution)/shard_map/in_proj_4/pallas_call | solution.py:157
  528.9 0.0 all-gather.20.cloned.1.call-done.refs_1_.refs_3_
  529.0 57.5 %out_proj_a.1.refs_2_ = f32[2048,2048]{1,0:T(8,128)} custom-call(bf16[16576,2048]{1,0:T(8,128)(2,1)} %in_proj_4.1.refs_0_, bf16[6144,2048]{1,0:T(8,128)(2,1)} %all-gather.20.cloned.1.call-done.refs_1_.refs_3_), custom_call_target="tpu_custom_call" | custom-call | flops 40802189312 | bytes 59768832 | tf_op jit(solution)/shard_map/out_proj_a/pallas_call | solution.py:325
  586.5 0.0 all-gather.18.cloned.1.call-done.refs_1_
  586.5 65.0 %out_proj_b.1 = bf16[2048,2048]{1,0:T(8,128)(2,1)} custom-call(bf16[16576,2048]{1,0:T(8,128)(2,1)} %in_proj_4.1.refs_0_, bf16[4096,2048]{1,0:T(8,128)(2,1)} %all-gather.18.cloned.1.call-done.refs_1_, f32[2048,2048]{1,0:T(8,128)} %out_proj_a.1.refs_2_, bf16[6144,2048]{1,0:T(8,128)(2,1)} %all-gather.20.cloned.1.call-done.refs_1_.refs_3_, ...), custom_call_target="tpu_custom_call" | custom-call | flops 45097156608 | bytes 66060288 | tf_op jit(solution)/shard_map/out_proj_b/pallas_call | solution.py:325
  (16 shorter events, 0.1 us)
Async XLA Ops:
  7.2 59.5 %all-gather.16.cloned.1.call-start = ((), (), s32[]{:S(2)}) async-start(), calls=%async_computation.4 | async-start | bytes 10813440 | tf_op jit(solution)/shard_map/all_gather | solution.py:375
  10.0 110.6 %all-gather.8.cloned.1.call-start = ((), (), s32[]{:S(2)}) async-start(), calls=%async_computation | async-start | bytes 10813440 | tf_op jit(solution)/shard_map/all_gather | solution.py:375
  12.2 177.8 %all-gather.14.cloned.1.call-start = ((), (), s32[]{:S(2)}) async-start(), calls=%async_computation.3 | async-start | bytes 17301504 | tf_op jit(solution)/shard_map/all_gather | solution.py:375
  13.4 245.9 %all-gather.12.cloned.1.call-start = ((), (), s32[]{:S(2)}) async-start(), calls=%async_computation.2 | async-start | bytes 17301504 | tf_op jit(solution)/shard_map/all_gather | solution.py:375
  14.0 388.0 %all-gather.10.cloned.1.call-start = ((), (), s32[]{:S(2)}) async-start(), calls=%async_computation.1 | async-start | bytes 23789568 | tf_op jit(solution)/shard_map/all_gather | solution.py:375
  15.1 513.9 %all-gather.20.cloned.1.call-start = ((), (), s32[]{:S(2)}) async-start(), calls=%async_computation.6 | async-start | bytes 25952256 | tf_op jit(solution)/shard_map/all_gather | solution.py:379
  17.3 569.2 %all-gather.18.cloned.1.call-start = ((), (), s32[]{:S(2)}) async-start(), calls=%async_computation.5 | async-start | bytes 17301504 | tf_op jit(solution)/shard_map/all_gather | solution.py:380
  19.4 10.6 %slice-start = ((s8[8388608]{0:T(1024)(128)(4,1)}), s8[4194304]{0:T(1024)(128)(4,1)S(1)}, s32[]{:S(2)}) async-start(s8[8388608]{0:T(1024)(128)(4,1)} %bitcast.31), calls=%async_computation.7 | async-start | bytes 8388608
  19.4 10.6 %copy-start.6 = (f32[2048]{0:T(1024)S(1)}, f32[2048]{0:T(1024)}, u32[]{:S(2)}) copy-start(f32[2048]{0:T(1024)} %param.5) | copy-start | bytes 24580
  24.1 5.9 slice-start.1
  193.2 73.0 %slice-start.2 = ((bf16[4096,2048]{1,0:T(8,128)(2,1)}), bf16[112,2048]{1,0:T(8,128)(2,1)S(1)}, s32[]{:S(2)}) async-start(bf16[4096,2048]{1,0:T(8,128)(2,1)} %all-gather.14.cloned.1.call-done.refs_0_), calls=%async_computation.9 | async-start | bytes 917504 | tf_op jit(solution)/shard_map/slice | solution.py:402
  193.2 73.0 %slice-start.3 = ((bf16[2560,2048]{1,0:T(8,128)(2,1)}), bf16[80,2048]{1,0:T(8,128)(2,1)S(1)}, s32[]{:S(2)}) async-start(bf16[2560,2048]{1,0:T(8,128)(2,1)} %all-gather.16.cloned.1.call-done.refs_0_), calls=%async_computation.10 | async-start | bytes 655360 | tf_op jit(solution)/shard_map/slice | solution.py:402
  285.6 2.8 copy-start.5
  319.3 42.1 %copy-start = (bf16[2048,1024]{1,0:T(8,128)(2,1)}, bf16[2048,1024]{1,0:T(8,128)(2,1)S(1)}, u32[]{:S(2)}) copy-start(bf16[2048,1024]{1,0:T(8,128)(2,1)S(1)} %get-tuple-element.6.refs_3_.refs_4_) | copy-start | bytes 12582916
  361.4 42.6 %slice-start.4 = ((bf16[2560,2048]{1,0:T(8,128)(2,1)}), bf16[320,2048]{1,0:T(8,128)(2,1)S(1)}, s32[]{:S(2)}) async-start(bf16[2560,2048]{1,0:T(8,128)(2,1)} %all-gather.8.cloned.1.call-done.refs_0_), calls=%async_computation.11 | async-start | bytes 2621440 | tf_op jit(solution)/shard_map/slice | solution.py:410
  404.5 11.9 %copy-start.2 = (bf16[2048,256]{1,0:T(8,128)(2,1)S(1)}, bf16[2048,256]{1,0:T(8,128)(2,1)}, u32[]{:S(2)}) copy-start(bf16[2048,256]{1,0:T(8,128)(2,1)} %get-tuple-element.7.k_ref) | copy-start | bytes 3145732
  404.6 11.9 %copy-start.3 = (bf16[2048,256]{1,0:T(8,128)(2,1)S(1)}, bf16[2048,256]{1,0:T(8,128)(2,1)}, u32[]{:S(2)}) copy-start(bf16[2048,256]{1,0:T(8,128)(2,1)} %get-tuple-element.8.v_ref) | copy-start | bytes 3145732
  416.5 29.1 %copy-start.1 = (bf16[2048,1024]{1,0:T(8,128)(2,1)S(1)}, bf16[2048,1024]{1,0:T(8,128)(2,1)}, u32[]{:S(2)}) copy-start(bf16[2048,1024]{1,0:T(8,128)(2,1)} %copy-done) | copy-start | bytes 12582916
  445.6 54.9 %copy-start.4 = (bf16[2048,1024]{1,0:T(8,128)(2,1)}, bf16[2048,1024]{1,0:T(8,128)(2,1)S(1)}, u32[]{:S(2)}) copy-start(bf16[2048,1024]{1,0:T(8,128)(2,1)S(1)} %mqa_b.1.refs_5_) | copy-start | bytes 12582916
Sparse Core Ops, SparseCore 0:
  10.2 56.5 all-gather.15
  68.8 51.7 all-gather.7
  123.3 66.7 all-gather.13
  192.6 66.6 all-gather.11
  261.2 81.0 all-gather.9
  344.4 86.0 all-gather.19
  432.5 66.6 all-gather.17

commit v2 on v1

--- a/solution.py
+++ b/solution.py
@@ -7,15 +7,11 @@
 from jax.experimental.pallas import tpu as pltpu
 from jax.sharding import PartitionSpec as P
 
+
+MESH = pl.DeviceIdType.MESH
+
 LN_EPS = 1e-6
 ROPE_BASE = 10000.0
-
-
-def layer_norm(x, ln_gain):
-    x_wide = x.astype(jnp.float32)
-    centered = x_wide - jnp.mean(x_wide, axis=-1, keepdims=True)
-    row_var = jnp.mean(centered * centered, axis=-1, keepdims=True)
-    return (centered * lax.rsqrt(row_var + LN_EPS) * ln_gain).astype(jnp.bfloat16)
 
 
 def rope_tables(seq_len, head_dim):
@@ -23,6 +19,188 @@
     inv_freq = ROPE_BASE ** (-jnp.arange(half, dtype=jnp.float32) * 2.0 / head_dim)
     angles = jnp.arange(seq_len, dtype=jnp.float32)[:, None] * inv_freq[None, :]
     return jnp.cos(angles), jnp.sin(angles)
+
+
+UNIT = 16
+
+
+class Ring:
+    def __init__(self, mesh_shape, shard_ref, out_ref, stage, lsem, sends, recvs, sib_sends, sib_recvs):
+        self.n = mesh_shape['tp']
+        self.size = mesh_shape['dp'] // 2 * self.n
+        assert mesh_shape['dp'] // 2 == self.n and self.size % 2 == 0
+        self.far = self.size // 2
+        self.shard, self.out, self.stage, self.lsem = shard_ref, out_ref, stage, lsem
+        self.sends, self.recvs, self.sib_sends, self.sib_recvs = sends, recvs, sib_sends, sib_recvs
+        self.rows = shard_ref.shape[0]
+        top = (self.rows // UNIT + 1) // 2 * UNIT
+        self.parts = ((0, top), (top, self.rows - top))
+        self.dp, self.tp = lax.axis_index('dp'), lax.axis_index('tp')
+        self.core = lax.rem(self.dp, 2)
+        x = lax.div(self.dp, 2)
+        a = x * (1 - self.core) + self.tp * self.core
+        other = self.tp * (1 - self.core) + x * self.core
+        self.pos = a * self.n + lax.rem(other + a, self.n)
+        self.sibling = {'dp': self.dp + 1 - 2 * self.core, 'tp': self.tp}
+
+    def at(self, pos):
+        pos = lax.rem(pos + 2 * self.size, self.size)
+        a = lax.div(pos, self.n)
+        other = lax.rem(lax.rem(pos, self.n) + (self.n - 1) * a, self.n)
+        x = a * (1 - self.core) + other * self.core
+        y = other * (1 - self.core) + a * self.core
+        return 2 * x + self.core, y
+
+    def device(self, pos):
+        dp, tp = self.at(pos)
+        return {'dp': dp, 'tp': tp}
+
+    def slot(self, pos, sub):
+        dp, tp = self.at(pos)
+        lo, n = self.parts[sub]
+        return self.out.at[pl.ds(pl.multiple_of((dp * self.n + tp) * self.rows + lo, UNIT), n), :]
+
+    def owner(self, way, t):
+        return self.pos - t if way == 0 else self.pos + t
+
+    def hop(self, way, t, sub):
+        lo, n = self.parts[sub]
+        dst = self.slot(self.owner(way, t - 1), sub)
+        src = dst
+        if isinstance(t, int) and t == 1:
+            src = self.shard.at[pl.ds(lo, n), :]
+        return pltpu.make_async_remote_copy(
+            src_ref=src, dst_ref=dst, send_sem=self.sends.at[way, t, sub], recv_sem=self.recvs.at[way, t, sub],
+            device_id=self.device(self.pos + 1 if way == 0 else self.pos - 1), device_id_type=MESH)
+
+    def across(self, way, t, sub):
+        lo, n = self.parts[sub]
+        dst = self.slot(self.owner(way, t), sub)
+        src = self.shard.at[pl.ds(lo, n), :] if isinstance(t, int) and t == 0 else dst
+        return pltpu.make_async_remote_copy(
+            src_ref=src, dst_ref=dst, send_sem=self.sib_sends.at[way, t, sub], recv_sem=self.sib_recvs.at[way, t, sub],
+            device_id=self.sibling, device_id_type=MESH)
+
+    def begin(self):
+        barrier = pltpu.get_barrier_semaphore()
+        for dev in (self.device(self.pos + 1), self.device(self.pos - 1), self.sibling):
+            pl.semaphore_signal(barrier, inc=1, device_id=dev, device_id_type=MESH)
+        pl.semaphore_wait(barrier, 3)
+        for sub in range(2):
+            for way in range(2):
+                self.hop(way, 1, sub).start()
+        for sub in range(2):
+            self.across(0, 0, sub).start()
+        pltpu.make_async_copy(self.shard, self.stage, self.lsem.at[0]).start()
+
+    def keep_own(self):
+        pltpu.make_async_copy(self.shard, self.stage, self.lsem.at[0]).wait()
+        dp, tp = self.at(self.pos)
+        mine = self.out.at[pl.ds(pl.multiple_of((dp * self.n + tp) * self.rows, UNIT), self.rows), :]
+        return pltpu.make_async_copy(self.stage, mine, self.lsem.at[1])
+
+    def event(self, t, sub):
+        def guard(cond, fn):
+            if isinstance(cond, bool):
+                if cond:
+                    fn()
+            else:
+                pl.when(cond)(fn)
+
+        for way in (0, 1):
+            far = self.far if way == sub else self.far - 1
+
+            def take(way=way, far=far):
+                self.hop(way, t, sub).wait_recv()
+                guard(t + 1 <= far, lambda: self.hop(way, t + 1, sub).start())
+                self.across(way, t, sub).start()
+
+            guard(t <= far, take)
+
+    def all_parts(self):
+        for t in range(1, self.far + 1):
+            for sub in range(2):
+                for way in ((sub,) if t == self.far else (0, 1)):
+                    yield way, t, sub
+
+    def finish(self):
+        for sub in range(2):
+            self.across(0, 0, sub).wait()
+        for way, t, sub in self.all_parts():
+            self.hop(way, t, sub).wait_send()
+            self.across(way, t, sub).wait()
+
+
+def ring_scratch(mesh_shape, rows, depth):
+    far = mesh_shape['dp'] // 2 * mesh_shape['tp'] // 2
+    return [pltpu.VMEM((rows, depth), jnp.bfloat16), pltpu.SemaphoreType.DMA((2,))] + [
+        pltpu.SemaphoreType.DMA((2, far + 1, 2))] * 4
+
+
+def norm_call(x, gain, shard, mesh_shape):
+    n_tok, d = x.shape
+    rows = shard.shape[0]
+    n_dev = mesh_shape['dp'] * mesh_shape['tp']
+    tt = 256
+    n_t = n_tok // tt
+
+    def body(x_ref, gain_ref, shard_ref, h_ref, ht_ref, out_ref, xbuf, hbuf, tbuf, xsem, hsem, tsem, *ring_refs):
+        ring = Ring(mesh_shape, shard_ref, out_ref, *ring_refs)
+
+        def load(i):
+            return pltpu.make_async_copy(x_ref.at[pl.ds(i * tt, tt), :], xbuf.at[i % 2], xsem.at[i % 2])
+
+        def put(i):
+            return [pltpu.make_async_copy(hbuf.at[i % 2], h_ref.at[pl.ds(i * tt, tt), :], hsem.at[i % 2]),
+                    pltpu.make_async_copy(tbuf.at[i % 2], ht_ref.at[:, pl.ds(i * tt, tt)], tsem.at[i % 2])]
+
+        load(0).start()
+        ring.begin()
+        own = None
+        events = [(t, sub) for t in range(1, ring.far + 1) for sub in range(2)]
+        per = len(events) // n_t
+        for i in range(n_t):
+            if i + 1 < n_t:
+                load(i + 1).start()
+            load(i).wait()
+            if i >= 2:
+                for c in put(i - 2):
+                    c.wait()
+            wide = xbuf[i % 2].astype(jnp.float32)
+            centered = wide - jnp.mean(wide, axis=-1, keepdims=True)
+            var = jnp.mean(centered * centered, axis=-1, keepdims=True)
+            h = centered * lax.rsqrt(var + LN_EPS) * gain_ref[...]
+            hbuf[i % 2] = h.astype(jnp.bfloat16)
+            tbuf[i % 2] = h.T.astype(jnp.bfloat16)
+            for c in put(i):
+                c.start()
+            if i == 0:
+                own = ring.keep_own()
+                own.start()
+            for ev in events[i * per:(i + 1) * per]:
+                ring.event(*ev)
+        for ev in events[n_t * per:]:
+            ring.event(*ev)
+        for i in (n_t - 2, n_t - 1):
+            for c in put(i):
+                c.wait()
+        own.wait()
+        ring.finish()
+
+    any_spec = pl.BlockSpec(memory_space=pl.ANY)
+    return pl.pallas_call(
+        body,
+        in_specs=[any_spec, pl.BlockSpec(memory_space=pltpu.VMEM), any_spec],
+        out_specs=[any_spec] * 3,
+        out_shape=[jax.ShapeDtypeStruct((n_tok, d), jnp.bfloat16), jax.ShapeDtypeStruct((d, n_tok), jnp.bfloat16),
+                   jax.ShapeDtypeStruct((n_dev * rows, d), jnp.bfloat16)],
+        scratch_shapes=[pltpu.VMEM((2, tt, d), jnp.bfloat16), pltpu.VMEM((2, tt, d), jnp.bfloat16),
+                        pltpu.VMEM((2, d, tt), jnp.bfloat16)] + [pltpu.SemaphoreType.DMA((2,))] * 3
+        + ring_scratch(mesh_shape, rows, d),
+        compiler_params=pltpu.CompilerParams(collective_id=0, has_side_effects=True, vmem_limit_bytes=40 * 1024 * 1024),
+        cost_estimate=pl.CostEstimate(flops=30 * 10 ** 9, bytes_accessed=n_tok * d * 6, transcendentals=0),
+        name="norm",
+    )(x, gain[None, :], shard)
 
 
 def attention_call(rows, k_arr, v_arr, cos_tab, sin_tab, n_heads, head_dim, fresh_k):
@@ -49,6 +227,7 @@
                     ks_ref[r, :] = rope(k_ref[r, :], cos_ref[r, :], sin_ref[r, :])
                     vs_ref[r, :] = v_ref[r, :]
                     return c
+
                 lax.fori_loop(0, n_len, one, 0)
 
         trow = pl.ds(pl.multiple_of(qi * tq, tq), tq)
@@ -101,48 +280,86 @@
     )(rows, k_arr, v_arr, cos_tab, sin_tab)
 
 
-def in_proj_call(chunk, h_t, p_t, dep, first, n_dev, block, offset, name):
+def in_proj_call(chunk, h_t, p_t, shard, first, mesh_shape, block, offset, collective_id):
+    n_dev = mesh_shape['dp'] * mesh_shape['tp']
     rows = chunk.shape[0] // n_dev
     depth, n_tok = h_t.shape
     n_grp = n_dev - first
-    g = next(c for c in (7, 4, 2, 1) if n_grp % c == 0)
+    g = next(c for c in (7, 4, 2, 1) if n_grp % c == 0 and c * rows <= 1280)
     steps = n_grp // g
     m = g * rows
-    tn = min(512, n_tok)
-    n_in = 2 + (p_t is not None) + (dep is not None)
+    tn = min(1024, n_tok)
+    n_n = n_tok // tn
+    n_in = 2 + (p_t is not None) + (shard is not None)
+    n_out = 1 + (shard is not None)
 
     def body(*refs):
         chunk_ref, h_ref = refs[0], refs[1]
-        out_ref, lbuf, obuf, lsem, osem = refs[n_in:]
+        out_ref = refs[n_in]
+        lbuf, obuf, lsem, osem = refs[n_in + n_out:n_in + n_out + 4]
+        ring = None
+        if shard is not None:
+            ring = Ring(mesh_shape, refs[n_in - 1], refs[n_in + 1], *refs[n_in + n_out + 4:])
 
         def load(s):
-            return pltpu.make_async_copy(chunk_ref.at[pl.ds(first * rows + s * m, m), :], lbuf.at[s % 2], lsem.at[s % 2])
+            slot = s % 2 if isinstance(s, int) else lax.rem(s, 2)
+            row = first * rows + s * m
+            row = row if isinstance(s, int) else pl.multiple_of(row, UNIT)
+            return pltpu.make_async_copy(chunk_ref.at[pl.ds(row, m), :], lbuf.at[slot], lsem.at[slot])
 
         def stores(s):
-            return [pltpu.make_async_copy(obuf.at[s % 2, pl.ds(i * rows, rows), :],
-                                          out_ref.at[pl.ds((s * g + i) * block + offset, rows), :],
-                                          osem.at[s % 2, i]) for i in range(g)]
+            slot = s % 2 if isinstance(s, int) else lax.rem(s, 2)
+            to = [(s * g + i) * block + offset for i in range(g)]
+            to = to if isinstance(s, int) else [pl.multiple_of(r, UNIT) for r in to]
+            return [pltpu.make_async_copy(obuf.at[slot, pl.ds(i * rows, rows), :], out_ref.at[pl.ds(to[i], rows), :],
+                                          osem.at[slot, i]) for i in range(g)]
 
         load(0).start()
-        for s in range(steps):
-            if s + 1 < steps:
-                load(s + 1).start()
-            load(s).wait()
-            if s >= 2:
-                for c in stores(s - 2):
-                    c.wait()
-
-            def tile(n, carry):
-                cols = pl.ds(pl.multiple_of(n * tn, tn), tn)
-                obuf[s % 2, :, cols] = jnp.dot(lbuf[s % 2], h_ref[:, cols],
-                                               preferred_element_type=jnp.float32).astype(jnp.bfloat16)
-                return carry
-            lax.fori_loop(0, n_tok // tn, tile, 0)
-            for c in stores(s):
-                c.start()
+        own = None
+        if ring is not None:
+            ring.begin()
+            own = ring.keep_own()
+            own.start()
+            assert steps * n_n == ring.far
+
+        def tick(it, carry):
+            s, n = lax.div(it, n_n), lax.rem(it, n_n)
+            slot = lax.rem(s, 2)
+
+            @pl.when(n == 0)
+            def _():
+                @pl.when(s + 1 < steps)
+                def _():
+                    load(s + 1).start()
+
+                load(s).wait()
+
+                @pl.when(s >= 2)
+                def _():
+                    for c in stores(s - 2):
+                        c.wait()
+
+            cols = pl.ds(pl.multiple_of(n * tn, tn), tn)
+            obuf[slot, :, cols] = jnp.dot(lbuf[slot], h_ref[:, cols],
+                                          preferred_element_type=jnp.float32).astype(jnp.bfloat16)
+            if ring is not None:
+                for sub in range(2):
+                    ring.event(it + 1, sub)
+
+            @pl.when(n == n_n - 1)
+            def _():
+                for c in stores(s):
+                    c.start()
+
+            return carry
+
+        lax.fori_loop(0, steps * n_n, tick, 0)
         for s in range(max(0, steps - 2), steps):
             for c in stores(s):
                 c.wait()
+        if ring is not None:
+            own.wait()
+            ring.finish()
 
     any_spec = pl.BlockSpec(memory_space=pl.ANY)
     args, specs, alias = [chunk, h_t], [any_spec, pl.BlockSpec(memory_space=pltpu.VMEM)], {}
@@ -150,22 +367,26 @@
         alias = {len(args): 0}
         args.append(p_t)
         specs.append(any_spec)
-    if dep is not None:
-        args.append(dep)
+    out_shape = [jax.ShapeDtypeStruct((n_grp * block, n_tok), jnp.bfloat16)]
+    scratch = [pltpu.VMEM((2, m, depth), jnp.bfloat16), pltpu.VMEM((2, m, n_tok), jnp.bfloat16),
+               pltpu.SemaphoreType.DMA((2,)), pltpu.SemaphoreType.DMA((2, g))]
+    kind = {}
+    if shard is not None:
+        args.append(shard)
         specs.append(any_spec)
-    total = n_grp * block
+        out_shape.append(jax.ShapeDtypeStruct((n_dev * shard.shape[0], depth), jnp.bfloat16))
+        scratch += ring_scratch(mesh_shape, shard.shape[0], depth)
+        kind = dict(collective_id=collective_id, has_side_effects=True)
     return pl.pallas_call(
         body,
         in_specs=specs,
-        out_specs=any_spec,
-        out_shape=jax.ShapeDtypeStruct((total, n_tok), jnp.bfloat16),
+        out_specs=[any_spec] * n_out,
+        out_shape=out_shape,
         input_output_aliases=alias,
-        scratch_shapes=[pltpu.VMEM((2, m, depth), jnp.bfloat16), pltpu.VMEM((2, m, n_tok), jnp.bfloat16),
-                        pltpu.SemaphoreType.DMA((2,)), pltpu.SemaphoreType.DMA((2, g))],
-        compiler_params=pltpu.CompilerParams(vmem_limit_bytes=48 * 1024 * 1024),
+        scratch_shapes=scratch,
+        compiler_params=pltpu.CompilerParams(vmem_limit_bytes=48 * 1024 * 1024, **kind),
         cost_estimate=pl.CostEstimate(flops=2 * n_grp * rows * depth * n_tok,
                                       bytes_accessed=2 * n_grp * rows * (depth + n_tok), transcendentals=0),
-        name=name,
     )(*args)
 
 
@@ -180,17 +401,17 @@
     first = sum(1 for z in range(q_pieces) if at <= z % per_dev < at + per)
     count = n_all - first
     steps, rest = divmod(count, full)
-    assert rest in (0, tail)
+    assert rest == tail and steps > 2
     kk = full * PIECE
     tt = min(512, n_tok)
     n_t = n_tok // tt
 
     def body(*refs):
         if last is None:
-            p_ref, w_ref, out_ref, acc_ref, gbuf, ubuf, wbuf, sem = refs
+            p_ref, w_ref, out_ref, acc_ref, gbuf, ubuf, wbuf, sem, osem = refs
         else:
             (p_ref, w_ref, accin_ref, w0_ref, a0_ref, a1_ref, x_ref, out_ref,
-             acc_ref, gbuf, ubuf, wbuf, sem, abuf, xbuf, asem, xsem, osem) = refs
+             acc_ref, gbuf, ubuf, wbuf, sem, osem, abuf, xbuf, asem, xsem) = refs
 
         def copies(s, slot, n):
             row = pl.multiple_of((first + s * full) * PIECE, PIECE) if not isinstance(s, int) else (first + s * full) * PIECE
@@ -218,9 +439,14 @@
             for c in copies(s, slot, n):
                 c.wait()
 
-        def mlp(slot, n, fresh):
+        def part(ref, t):
+            return ref.at[pl.ds(t * tt, tt), :]
+
+        def mlp(slot, n, fresh, before=None, after=None):
             k = n * PIECE
             for t in range(n_t):
+                if before is not None:
+                    before(t)
                 tok = slice(t * tt, (t + 1) * tt)
                 g = gbuf[slot, 0:k, tok].astype(jnp.float32)
                 u = ubuf[slot, 0:k, tok].astype(jnp.float32)
@@ -230,19 +456,20 @@
                     acc_ref[tok, :] = prod
                 else:
                     acc_ref[tok, :] += prod
+                if after is not None:
+                    after(t)
 
         start(0, 0, full)
         if last is not None:
-            acc_in = pltpu.make_async_copy(accin_ref, acc_ref, xsem.at[0])
-            acc_in.start()
-            x_in = pltpu.make_async_copy(x_ref, xbuf, xsem.at[1])
+            acc_in = [pltpu.make_async_copy(part(accin_ref, t), part(acc_ref, t), osem.at[t]) for t in range(n_t)]
+            for c in acc_in:
+                c.start()
+            x_in = pltpu.make_async_copy(x_ref, xbuf, xsem.at[0])
             x_in.start()
-            acc_in.wait()
-        else:
-            start(1, 1, full)
-            finish(0, 0, full)
-            mlp(0, full, True)
-        lo = 0 if last is not None else 1
+        start(1, 1, full)
+        finish(0, 0, full)
+        mlp(0, full, last is None, (lambda t: acc_in[t].wait()) if last is not None else None)
+        lo = 1
 
         def step(s, carry):
             slot = lax.rem(s, 2)
@@ -250,10 +477,11 @@
             @pl.when(s + 1 < steps)
             def _():
                 start(s + 1, 1 - slot, full)
-            if rest:
-                @pl.when(s + 1 == steps)
-                def _():
-                    start(steps, 1 - slot, tail)
+
+            @pl.when(s + 1 == steps)
+            def _():
+                start(steps, 1 - slot, tail)
+
             finish(s, slot, full)
             mlp(slot, full, False)
             return carry
@@ -265,7 +493,7 @@
 
             def attn_copies(i):
                 ref, blk, odd = srcs[i]
-                slot = i % 2
+                slot = (i + steps + 1) % 2
                 res = [pltpu.make_async_copy(ref.at[:, pl.ds(blk * kk, kk)], abuf.at[slot], asem.at[slot, 0])]
                 for j in range(full):
                     half, r = divmod(j, full // 2)
@@ -279,47 +507,51 @@
                     res.append(pltpu.make_async_copy(src, wbuf.at[slot, pl.ds(j * PIECE, PIECE), :], asem.at[slot, 1 + j]))
                 return res
 
-        if rest:
-            finish(steps, steps % 2, tail)
-            mlp(steps % 2, tail, False)
-
-        if last is None:
-            out = pltpu.make_async_copy(acc_ref, out_ref, sem.at[0, 0])
-            out.start()
-            out.wait()
-        else:
-            for c in attn_copies(0):
+            attn_copies_0 = attn_copies(0)
+            for c in attn_copies_0:
                 c.start()
+        outs = []
+
+        def put(src, t, sems):
+            c = pltpu.make_async_copy(part(src, t), part(out_ref, t), sems.at[t])
+            c.start()
+            outs.append(c)
+
+        finish(steps, steps % 2, tail)
+        mlp(steps % 2, tail, False, None, (lambda t: put(acc_ref, t, osem)) if last is None else None)
+
+        if last is not None:
             for i in range(len(srcs)):
                 if i + 1 < len(srcs):
                     for c in attn_copies(i + 1):
                         c.start()
                 for c in attn_copies(i):
                     c.wait()
+                slot = (i + steps + 1) % 2
+                if i + 1 == len(srcs):
+                    x_in.wait()
                 for t in range(n_t):
                     tok = slice(t * tt, (t + 1) * tt)
-                    acc_ref[tok, :] += jnp.dot(abuf[i % 2, tok, :], wbuf[i % 2], preferred_element_type=jnp.float32)
-            x_in.wait()
-            outs = []
-            for t in range(n_t):
-                tok = slice(t * tt, (t + 1) * tt)
-                xbuf[tok, :] = (xbuf[tok, :].astype(jnp.float32) + acc_ref[tok, :]).astype(jnp.bfloat16)
-                c = pltpu.make_async_copy(xbuf.at[pl.ds(t * tt, tt), :], out_ref.at[pl.ds(t * tt, tt), :], osem.at[t])
-                c.start()
-                outs.append(c)
-            for c in outs:
-                c.wait()
+                    total = acc_ref[tok, :] + jnp.dot(abuf[slot, tok, :], wbuf[slot], preferred_element_type=jnp.float32)
+                    if i + 1 < len(srcs):
+                        acc_ref[tok, :] = total
+                    else:
+                        xbuf[tok, :] = (xbuf[tok, :].astype(jnp.float32) + total).astype(jnp.bfloat16)
+                        put(xbuf, t, osem)
+        for c in outs:
+            c.wait()
 
     any_spec = pl.BlockSpec(memory_space=pl.ANY)
     args = [p_t, w_chunk]
     scratch = [pltpu.VMEM((n_tok, d_out), jnp.float32)] + [pltpu.VMEM((2, kk, n_tok), jnp.bfloat16)] * 2
-    scratch += [pltpu.VMEM((2, kk, d_out), jnp.bfloat16), pltpu.SemaphoreType.DMA((2, 1 + 2 * full))]
+    scratch += [pltpu.VMEM((2, kk, d_out), jnp.bfloat16), pltpu.SemaphoreType.DMA((2, 1 + 2 * full)),
+                pltpu.SemaphoreType.DMA((n_t,))]
     out_dtype = jnp.float32
     if last is not None:
         w_first, a0, a1, x = last
         args += [acc, w_first, a0, a1, x]
         scratch += [pltpu.VMEM((2, n_tok, kk), jnp.bfloat16), pltpu.VMEM((n_tok, d_out), jnp.bfloat16),
-                    pltpu.SemaphoreType.DMA((2, 1 + full)), pltpu.SemaphoreType.DMA((2,)), pltpu.SemaphoreType.DMA((n_t,))]
+                    pltpu.SemaphoreType.DMA((2, 1 + full)), pltpu.SemaphoreType.DMA((1,))]
         out_dtype = jnp.bfloat16
     k_total = count * PIECE + (q_width if last is not None else 0)
     return pl.pallas_call(
@@ -334,16 +566,18 @@
     )(*args)
 
 
-UNIT = 16
 EARLY_UNITS = (5, 8, 8)
-LATE_UNITS = (11, 5)
 FIRST_PIECES = 3
 
 
 def solution(mesh):
     tok_spec = P(('part', 'dp', 'tp'))
     group = ('dp', 'tp')
-    n_dev = mesh.shape['dp'] * mesh.shape['tp']
+    mesh_shape = dict(mesh.shape)
+    n_dev = mesh_shape['dp'] * mesh_shape['tp']
+
+    def gather(shard):
+        return lax.all_gather(shard, group, axis=0, tiled=True)
 
     def per_device(x_blk, ln_gain, w_in_blk, w_out_blk):
         x = x_blk[0]
@@ -360,42 +594,35 @@
         early_rows = block - head_dim
         cuts = [(2 * d + 1) * head_dim - d * block for d in range(first)]
         assert 2 * first == n_heads and all(0 <= c <= early_rows for c in cuts)
-        assert sum(EARLY_UNITS) * UNIT == early_rows and sum(LATE_UNITS) * UNIT == head_dim
+        assert sum(EARLY_UNITS) * UNIT == early_rows
         w_rows = w_in_blk.T
-        me = lax.axis_index('dp') * mesh.shape['tp'] + lax.axis_index('tp')
+        me = lax.axis_index('dp') * mesh_shape['tp'] + lax.axis_index('tp')
         cut = jnp.where(me < first, head_dim - (block - 2 * head_dim) * me, early_rows)
         below = lax.broadcasted_iota(jnp.int32, (early_rows, 1), 0) < cut
         early_local = jnp.where(below, w_rows[:early_rows], w_rows[head_dim:])
         late_local = lax.dynamic_slice_in_dim(w_rows, cut, head_dim, axis=0)
-
-        chunks, offset = [], 0
-        for local, units in ((early_local, EARLY_UNITS), (late_local, LATE_UNITS)):
-            at = 0
-            for u in units:
-                chunks.append((lax.all_gather(local[at:at + u * UNIT], group, axis=0, tiled=True), offset))
-                at += u * UNIT
-                offset += u * UNIT
-        cut_out = FIRST_PIECES * PIECE
-        w_out_a = lax.all_gather(w_out_blk[:cut_out], group, axis=0, tiled=True)
-        w_out_b = lax.all_gather(w_out_blk[cut_out:], group, axis=0, tiled=True)
-
-        h = layer_norm(x, ln_gain)
-        h_t = h.T
+        shards, at = [], 0
+        for u in EARLY_UNITS:
+            shards.append(early_local[at:at + u * UNIT])
+            at += u * UNIT
+
+        h, h_t, c0 = norm_call(x, ln_gain, shards[0], mesh_shape)
         cos_tab, sin_tab = rope_tables(seq_len, head_dim)
-
-        def head_rows(parts):
-            return jnp.concatenate([c.reshape(n_dev, -1, d_model) for c, _ in parts], axis=1)
 
         def project(w):
             return lax.dot_general(h, w, (((1,), (1,)), ((), ())), preferred_element_type=jnp.float32).astype(jnp.bfloat16)
 
-        n_early = len(EARLY_UNITS)
-        p_t = None
-        for i, (c, off) in enumerate(chunks[:n_early]):
-            p_t = in_proj_call(c, h_t, p_t, None, first, n_dev, block, off, f"in_proj_{i}")
-        tops = [c.reshape(n_dev, -1, d_model)[:first] for c, _ in chunks[:n_early]]
+        offs = [sum(EARLY_UNITS[:i]) * UNIT for i in range(len(EARLY_UNITS) + 1)]
+        p_t, c1 = in_proj_call(c0, h_t, None, shards[1], first, mesh_shape, block, offs[0], 1)
+        late = gather(late_local)
+        w_out_a = gather(w_out_blk[:FIRST_PIECES * PIECE])
+        w_out_b = gather(w_out_blk[FIRST_PIECES * PIECE:])
+        p_t, c2 = in_proj_call(c1, h_t, p_t, shards[2], first, mesh_shape, block, offs[1], 2)
+        p_t = in_proj_call(c2, h_t, p_t, None, first, mesh_shape, block, offs[2], None)[0]
+        early = (c0, c1, c2)
+        tops = [c.reshape(n_dev, -1, d_model)[:first] for c in early]
         rest, left = [], gate_at
-        for c, _ in chunks[:n_early]:
+        for c in early:
             per = c.shape[0] // n_dev
             take = min(left, per)
             if take:
@@ -403,14 +630,9 @@
             left -= take
         w_a = jnp.concatenate([jnp.concatenate(tops, axis=1).reshape(-1, d_model)] + rest, axis=0)
         attn_a, k_rot, v_all = attention_call(project(w_a), None, None, cos_tab, sin_tab, n_heads // 2, head_dim, True)
-        dep = attn_a
-        for i, (c, off) in enumerate(chunks[n_early:]):
-            p_t = in_proj_call(c, h_t, p_t, dep, first, n_dev, block, off, f"in_proj_{n_early + i}")
-            dep = None
-        tops = [c.reshape(n_dev, -1, d_model)[:first] for c, _ in chunks[n_early:]]
-        w_b = jnp.concatenate(tops, axis=1).reshape(-1, d_model)
-        attn_b = attention_call(project(w_b), k_rot, v_all, cos_tab, sin_tab, n_heads // 2, head_dim, False)[0]
-
+        p_t = in_proj_call(late, h_t, p_t, None, first, mesh_shape, block, offs[3], None)[0]
+        attn_b = attention_call(project(late[:first * head_dim]), k_rot, v_all, cos_tab, sin_tab, n_heads // 2,
+                                head_dim, False)[0]
         per_dev = out_block // PIECE
         acc = out_proj_call(p_t, w_out_a, 0, FIRST_PIECES, per_dev, q_width, gate_at, ff, None, None)
         y = out_proj_call(p_t, w_out_b, FIRST_PIECES, per_dev - FIRST_PIECES, per_dev, q_width, gate_at, ff, acc,

time: 664 us -> 662 us (level)
  Pallas kernels: 377 us -> 577 us
  waiting for transfers between devices: 175 us -> 0.22 us
  other arithmetic: 27.4 us -> 9.67 us
  local copies, waits for them, and re-layouts: 32.8 us -> 21.1 us
    pallas_call x5, Pallas kernels: 194 us -> 398 us  [the longest x4 315 us: in_proj_call(): pl.pallas_call(body, in_specs=specs, out_specs=[any_spec] * n_out, out_sh...]
    all_gather x7 -> x3, waiting for transfers between devices: 174 us -> 0.06 us  [gather(): return lax.all_gather(shard, group, axis=0, tiled=True)]
    transpose x1 -> x0, local copies, waits for them, and re-layouts: 11.8 us -> none  [per_device(): h_t = h.T]
    reduce_sum x2 -> x0, other arithmetic: 10.5 us -> none  [the longest x1 5.84 us: layer_norm(): row_var = jnp.mean(centered * centered, axis=-1, keepdims=True)]
    slice x12 -> x7, local copies, waits for them, and re-layouts: 16.9 us -> 9.12 us  [the longest x3 5.04 us: per_device(): tops = [c.reshape(n_dev, -1, d_model)[:first] for c in early]]
  transfers between devices with their start and end apart: 7 -> 3, of which waited for: 4 -> 0; matrix products, arithmetic and copies ran while one was open for 13% -> 8% of each run, Pallas kernels for 47% -> 79%
where the time goes in v2:
time: 662 us; the launch traced here: 653 us
  Pallas kernels  577 us (87%)
  matrix products  30.5 us (5%)
  local copies, waits for them, and re-layouts  21.1 us (3%)
  between operations  14.2 us (2%)
  other arithmetic  9.67 us (1%)
    pallas_call x4, Pallas kernels, in_proj_call(): pl.pallas_call(body, in_specs=specs, out_specs=[any_spec] * n_out, out_sh...  315 us
    pallas_call x2, Pallas kernels, out_proj_call(): pl.pallas_call(body, in_specs=[any_spec] * len(args), out_specs=any_spec,...  118 us
    pallas_call x1, Pallas kernels, norm_call(): pl.pallas_call(body, in_specs=[any_spec, pl.BlockSpec(memory_space=pltpu....  82.3 us
    pallas_call x2, Pallas kernels, attention_call(): pl.pallas_call(body, grid=(n_q, n_heads // pair), in_specs=[pl.BlockSpec(...  61.2 us
    dot_general x2, matrix products, project(): lax.dot_general(h, w, (((1,), (1,)), ((), ())), preferred_element_type=jn...  30.5 us
  transfers between devices with their start and end apart: 3, of which 0 were waited for; matrix products, arithmetic and copies ran while one was open for 8% of the time, Pallas kernels for 79%

profile of v2, /device:TPU:97, one launch (start us, length us, event | category | flops | bytes accessed | tf_op | source)
XLA Modules:
  0.0 652.7 jit_solution(10337980007064486791)
XLA Ops:
  7.2 0.0 copy-start.6
  7.2 0.0 copy-start
  7.2 0.1 all-gather.4.cloned.1.call-start
  7.3 2.5 dynamic-slice_bitcast_fusion
  9.8 0.1 all-gather.4.cloned.1.call-update
  9.8 0.1 all-gather.8.cloned.1.call-start
  9.9 2.1 slice.54
  12.0 0.1 all-gather.8.cloned.1.call-update
  12.1 0.1 all-gather.6.cloned.1.call-start
  12.2 1.9 slice.53
  14.0 0.1 all-gather.6.cloned.1.call-update
  14.1 0.0 copy-done.6
  14.1 0.2 slice_select_fusion
  14.4 0.0 copy-done
  14.4 82.3 %norm.1 = (bf16[2048,2048]{1,0:T(8,128)(2,1)S(1)}, bf16[2048,2048]{1,0:T(8,128)(2,1)}, bf16[2560,2048]{1,0:T(8,128)(2,1)}) custom-call(bf16[2048,2048]{1,0:T(8,128)(2,1)} %bitcast.22, f32[1,2048]{1,0:T(1,128)S(1)} %bitcast.14, bf16[80,2048]{1,0:T(8,128)(2,1)S(1)} %slice.66.shard_ref), custom_call_target="tpu_custom_call" | custom-call | flops 30000001024 | bytes 25165824 | tf_op jit(solution)/shard_map/norm/pallas_call | solution.py:191
  96.6 0.0 copy-start.5
  96.7 3.4 copy-done.5
  100.1 1.4 slice.55
  101.5 0.1 fusion.13
  101.6 99.1 %shard_map.67 = (bf16[16576,2048]{1,0:T(8,128)(2,1)}, bf16[4096,2048]{1,0:T(8,128)(2,1)}) custom-call(bf16[2560,2048]{1,0:T(8,128)(2,1)} %get-tuple-element.14.refs_0_, bf16[2048,2048]{1,0:T(8,128)(2,1)} %get-tuple-element.13.refs_1_, bf16[128,2048]{1,0:T(8,128)(2,1)S(1)} %get-tuple-element.24.refs_2_), custom_call_target="tpu_custom_call" | custom-call | flops 18790481920 | bytes 18350080 | tf_op jit(solution)/shard_map/pallas_call | solution.py:380
  200.7 1.8 slice.57
  202.6 1.1 slice.62
  203.6 1.0 slice.61
  204.6 106.0 %shard_map.68 = (bf16[16576,2048]{1,0:T(8,128)(2,1)}, bf16[4096,2048]{1,0:T(8,128)(2,1)}) custom-call(bf16[4096,2048]{1,0:T(8,128)(2,1)} %get-tuple-element.15.refs_0_, bf16[2048,2048]{1,0:T(8,128)(2,1)} %get-tuple-element.13.refs_1_, bf16[16576,2048]{1,0:T(8,128)(2,1)} %get-tuple-element.16.refs_2_, ...), custom_call_target="tpu_custom_call", output_to_operand_aliasing={{0}: (2, {})} | custom-call | flops 30064771072 | bytes 29360128 | tf_op jit(solution)/shard_map/pallas_call | solution.py:380
  310.6 1.8 slice.59
  312.4 5.6 pad_maximum_fusion
  318.0 3.9 fusion.10
  321.8 17.9 %convolution_convert_fusion.q_ref.k_ref.v_ref = bf16[2048,1536]{1,0:T(8,128)(2,1)S(1)} fusion(bf16[2048,2048]{1,0:T(8,128)(2,1)} %copy-done.5, bf16[112,2048]{1,0:T(8,128)(2,1)S(1)} %slice.62, bf16[80,2048]{1,0:T(8,128)(2,1)S(1)} %slice.61, bf16[1344,2048]{1,0:T(8,128)(2,1)} %bitcast.20), kind=kOutput, calls=%fused_computation | convolution fusion | flops 12906921984 | bytes 20971520 | tf_op jit(solution)/shard_map/dot_general | solution.py:613
  339.7 30.9 %mqa_a.1 = (bf16[2048,1024]{1,0:T(8,128)(2,1)S(1)}, bf16[2048,256]{1,0:T(8,128)(2,1)}, bf16[2048,256]{1,0:T(8,128)(2,1)}) custom-call(bf16[2048,1536]{1,0:T(8,128)(2,1)S(1)} %convolution_convert_fusion.q_ref.k_ref.v_ref, bf16[2048,1536]{1,0:T(8,128)(2,1)S(1)} %convolution_convert_fusion.q_ref.k_ref.v_ref, ...), custom_call_target="tpu_custom_call" | custom-call | flops 10737418240 | bytes 16777216 | tf_op jit(solution)/shard_map/mqa_a/pallas_call | solution.py:270
  370.6 0.0 copy-start.3
  370.6 2.1 copy-done.3
  372.7 39.4 %shard_map.69.refs_2_ = bf16[16576,2048]{1,0:T(8,128)(2,1)} custom-call(bf16[4096,2048]{1,0:T(8,128)(2,1)} %get-tuple-element.17.refs_0_, bf16[2048,2048]{1,0:T(8,128)(2,1)} %get-tuple-element.13.refs_1_, bf16[16576,2048]{1,0:T(8,128)(2,1)} %get-tuple-element.18.refs_2_), custom_call_target="tpu_custom_call", output_to_operand_aliasing={{}: (2, {})} | custom-call | flops 30064771072 | bytes 29360128 | tf_op jit(solution)/shard_map/pallas_call | solution.py:380
  412.1 0.0 copy-start.1
  412.1 0.0 all-gather.4.cloned.1.call-done.refs_0_
  412.2 0.0 copy-start.2
  412.2 12.7 %fusion.7.q_ref = bf16[2048,1024]{1,0:T(8,128)(2,1)S(1)} fusion(bf16[2048,2048]{1,0:T(8,128)(2,1)} %copy-done.5, bf16[8192,2048]{1,0:T(8,128)(2,1)} %all-gather.4.cloned.1.call-done.refs_0_), kind=kOutput, calls=%fused_computation.9 | convolution fusion | flops 8592031744 | bytes 16777216 | tf_op jit(solution)/shard_map/dot_general | solution.py:613
  424.8 0.0 copy-done.1
  424.9 0.0 copy-done.2
  424.9 30.3 %mqa_b.1.refs_5_ = bf16[2048,1024]{1,0:T(8,128)(2,1)S(1)} custom-call(bf16[2048,1024]{1,0:T(8,128)(2,1)S(1)} %fusion.7.q_ref, bf16[2048,256]{1,0:T(8,128)(2,1)S(1)} %copy-done.1, bf16[2048,256]{1,0:T(8,128)(2,1)S(1)} %copy-done.2, f32[2048,128]{1,0:T(8,128)S(1)} %get-tuple-element.26.cos_ref, f32[2048,128]{1,0:T(8,128)S(1)} %get-tuple-element.25.sin_ref), custom_call_target="tpu_custom_call" | custom-call | flops 10737418240 | bytes 16777216 | tf_op jit(solution)/shard_map/mqa_b/pallas_call | solution.py:270
  455.2 0.0 copy-start.4
  455.2 1.9 copy-done.4
  457.1 70.8 %shard_map.70.refs_0_ = bf16[16576,2048]{1,0:T(8,128)(2,1)} custom-call(bf16[8192,2048]{1,0:T(8,128)(2,1)} %all-gather.4.cloned.1.call-done.refs_0_, bf16[2048,2048]{1,0:T(8,128)(2,1)} %get-tuple-element.13.refs_1_, bf16[16576,2048]{1,0:T(8,128)(2,1)} %shard_map.69.refs_2_), custom_call_target="tpu_custom_call", output_to_operand_aliasing={{}: (2, {})} | custom-call | flops 60129542144 | bytes 58720256 | tf_op jit(solution)/shard_map/pallas_call | solution.py:380
  528.0 0.0 all-gather.8.cloned.1.call-done.refs_1_.refs_3_
  528.0 56.8 %out_proj_a.1.refs_2_ = f32[2048,2048]{1,0:T(8,128)} custom-call(bf16[16576,2048]{1,0:T(8,128)(2,1)} %shard_map.70.refs_0_, bf16[6144,2048]{1,0:T(8,128)(2,1)} %all-gather.8.cloned.1.call-done.refs_1_.refs_3_), custom_call_target="tpu_custom_call" | custom-call | flops 40802189312 | bytes 59768832 | tf_op jit(solution)/shard_map/out_proj_a/pallas_call | solution.py:557
  584.8 0.0 all-gather.6.cloned.1.call-done.refs_1_
  584.9 61.1 %out_proj_b.1 = bf16[2048,2048]{1,0:T(8,128)(2,1)} custom-call(bf16[16576,2048]{1,0:T(8,128)(2,1)} %shard_map.70.refs_0_, bf16[4096,2048]{1,0:T(8,128)(2,1)} %all-gather.6.cloned.1.call-done.refs_1_, f32[2048,2048]{1,0:T(8,128)} %out_proj_a.1.refs_2_, bf16[6144,2048]{1,0:T(8,128)(2,1)} %all-gather.8.cloned.1.call-done.refs_1_.refs_3_, ...), custom_call_target="tpu_custom_call" | custom-call | flops 45097156608 | bytes 66060288 | tf_op jit(solution)/shard_map/out_proj_b/pallas_call | solution.py:557
  (3 shorter events, 0.0 us)
Async XLA Ops:
  7.2 6.9 %copy-start.6 = (bf16[2048,592]{0,1:T(8,128)(2,1)S(1)}, bf16[2048,592]{0,1:T(8,128)(2,1)}, u32[]{:S(2)}) copy-start(bf16[2048,592]{0,1:T(8,128)(2,1)} %param.6) | copy-start | bytes 7274500
  7.2 7.2 %copy-start = (f32[2048]{0:T(1024)S(1)}, f32[2048]{0:T(1024)}, u32[]{:S(2)}) copy-start(f32[2048]{0:T(1024)} %param.5) | copy-start | bytes 24580
  7.2 404.9 %all-gather.4.cloned.1.call-start = ((), (), s32[]{:S(2)}) async-start(), calls=%async_computation | async-start | bytes 34603008 | tf_op jit(solution)/shard_map/all_gather | solution.py:580
  9.8 518.1 %all-gather.8.cloned.1.call-start = ((), (), s32[]{:S(2)}) async-start(), calls=%async_computation.2 | async-start | bytes 25952256 | tf_op jit(solution)/shard_map/all_gather | solution.py:580
  12.1 572.8 %all-gather.6.cloned.1.call-start = ((), (), s32[]{:S(2)}) async-start(), calls=%async_computation.1 | async-start | bytes 17301504 | tf_op jit(solution)/shard_map/all_gather | solution.py:580
  96.6 3.4 copy-start.5
  370.6 2.1 copy-start.3
  412.1 12.7 %copy-start.1 = (bf16[2048,256]{1,0:T(8,128)(2,1)S(1)}, bf16[2048,256]{1,0:T(8,128)(2,1)}, u32[]{:S(2)}) copy-start(bf16[2048,256]{1,0:T(8,128)(2,1)} %get-tuple-element.21.k_ref) | copy-start | bytes 3145732
  412.2 12.7 %copy-start.2 = (bf16[2048,256]{1,0:T(8,128)(2,1)S(1)}, bf16[2048,256]{1,0:T(8,128)(2,1)}, u32[]{:S(2)}) copy-start(bf16[2048,256]{1,0:T(8,128)(2,1)} %get-tuple-element.22.v_ref) | copy-start | bytes 3145732
  455.2 1.9 copy-start.4
Sparse Core Ops, SparseCore 0:
  10.1 144.3 all-gather.3
  156.7 110.1 all-gather.7
  268.9 70.2 all-gather.5

commit v3 on v2

--- a/solution.py
+++ b/solution.py
@@ -141,7 +141,7 @@
     n_tok, d = x.shape
     rows = shard.shape[0]
     n_dev = mesh_shape['dp'] * mesh_shape['tp']
-    tt = 256
+    tt = 128
     n_t = n_tok // tt
 
     def body(x_ref, gain_ref, shard_ref, h_ref, ht_ref, out_ref, xbuf, hbuf, tbuf, xsem, hsem, tsem, *ring_refs):
@@ -288,7 +288,7 @@
     g = next(c for c in (7, 4, 2, 1) if n_grp % c == 0 and c * rows <= 1280)
     steps = n_grp // g
     m = g * rows
-    tn = min(1024, n_tok)
+    tn = min(512, n_tok) if shard is not None else min(1024, n_tok)
     n_n = n_tok // tn
     n_in = 2 + (p_t is not None) + (shard is not None)
     n_out = 1 + (shard is not None)
@@ -320,7 +320,7 @@
             ring.begin()
             own = ring.keep_own()
             own.start()
-            assert steps * n_n == ring.far
+            assert steps * n_n == 2 * ring.far
 
         def tick(it, carry):
             s, n = lax.div(it, n_n), lax.rem(it, n_n)
@@ -344,7 +344,9 @@
                                           preferred_element_type=jnp.float32).astype(jnp.bfloat16)
             if ring is not None:
                 for sub in range(2):
-                    ring.event(it + 1, sub)
+                    @pl.when(lax.rem(it, 2) == sub)
+                    def _(sub=sub):
+                        ring.event(lax.div(it, 2) + 1, sub)
 
             @pl.when(n == n_n - 1)
             def _():

time: 662 us -> 658 us (level)
  no operation moved by 1% of the time
where the time goes in v3:
time: 658 us; the launch traced here: 648 us
  Pallas kernels  572 us (87%)
  matrix products  30.5 us (5%)
  local copies, waits for them, and re-layouts  21.1 us (3%)
  between operations  14.2 us (2%)
  other arithmetic  9.67 us (1%)
    pallas_call x4, Pallas kernels, in_proj_call(): pl.pallas_call(body, in_specs=specs, out_specs=[any_spec] * n_out, out_sh...  311 us
    pallas_call x2, Pallas kernels, out_proj_call(): pl.pallas_call(body, in_specs=[any_spec] * len(args), out_specs=any_spec,...  118 us
    pallas_call x1, Pallas kernels, norm_call(): pl.pallas_call(body, in_specs=[any_spec, pl.BlockSpec(memory_space=pltpu....  82.3 us
    pallas_call x2, Pallas kernels, attention_call(): pl.pallas_call(body, grid=(n_q, n_heads // pair), in_specs=[pl.BlockSpec(...  61.2 us
    dot_general x2, matrix products, project(): lax.dot_general(h, w, (((1,), (1,)), ((), ())), preferred_element_type=jn...  30.5 us
  transfers between devices with their start and end apart: 3, of which 0 were waited for; matrix products, arithmetic and copies ran while one was open for 8% of the time, Pallas kernels for 79%

profile of v3, /device:TPU:97, one launch (start us, length us, event | category | flops | bytes accessed | tf_op | source)
XLA Modules:
  0.0 648.1 jit_solution(15371004168503466477)
XLA Ops:
  7.2 0.0 copy-start.6
  7.2 0.0 copy-start
  7.2 0.1 all-gather.4.cloned.1.call-start
  7.3 2.5 dynamic-slice_bitcast_fusion
  9.8 0.1 all-gather.4.cloned.1.call-update
  9.8 0.1 all-gather.8.cloned.1.call-start
  9.9 2.1 slice.54
  12.0 0.1 all-gather.8.cloned.1.call-update
  12.1 0.1 all-gather.6.cloned.1.call-start
  12.2 1.9 slice.53
  14.0 0.1 all-gather.6.cloned.1.call-update
  14.1 0.0 copy-done.6
  14.1 0.2 slice_select_fusion
  14.4 0.0 copy-done
  14.4 82.3 %norm.1 = (bf16[2048,2048]{1,0:T(8,128)(2,1)S(1)}, bf16[2048,2048]{1,0:T(8,128)(2,1)}, bf16[2560,2048]{1,0:T(8,128)(2,1)}) custom-call(bf16[2048,2048]{1,0:T(8,128)(2,1)} %bitcast.22, f32[1,2048]{1,0:T(1,128)S(1)} %bitcast.14, bf16[80,2048]{1,0:T(8,128)(2,1)S(1)} %slice.66.shard_ref), custom_call_target="tpu_custom_call" | custom-call | flops 30000001024 | bytes 25165824 | tf_op jit(solution)/shard_map/norm/pallas_call | solution.py:191
  96.6 0.0 copy-start.5
  96.7 3.4 copy-done.5
  100.1 1.4 slice.55
  101.5 0.1 fusion.13
  101.6 99.1 %shard_map.67 = (bf16[16576,2048]{1,0:T(8,128)(2,1)}, bf16[4096,2048]{1,0:T(8,128)(2,1)}) custom-call(bf16[2560,2048]{1,0:T(8,128)(2,1)} %get-tuple-element.14.refs_0_, bf16[2048,2048]{1,0:T(8,128)(2,1)} %get-tuple-element.13.refs_1_, bf16[128,2048]{1,0:T(8,128)(2,1)S(1)} %get-tuple-element.24.refs_2_), custom_call_target="tpu_custom_call" | custom-call | flops 18790481920 | bytes 18350080 | tf_op jit(solution)/shard_map/pallas_call | solution.py:382
  200.7 1.8 slice.57
  202.6 1.1 slice.62
  203.6 1.0 slice.61
  204.6 101.3 %shard_map.68 = (bf16[16576,2048]{1,0:T(8,128)(2,1)}, bf16[4096,2048]{1,0:T(8,128)(2,1)}) custom-call(bf16[4096,2048]{1,0:T(8,128)(2,1)} %get-tuple-element.15.refs_0_, bf16[2048,2048]{1,0:T(8,128)(2,1)} %get-tuple-element.13.refs_1_, bf16[16576,2048]{1,0:T(8,128)(2,1)} %get-tuple-element.16.refs_2_, ...), custom_call_target="tpu_custom_call", output_to_operand_aliasing={{0}: (2, {})} | custom-call | flops 30064771072 | bytes 29360128 | tf_op jit(solution)/shard_map/pallas_call | solution.py:382
  306.0 1.8 slice.59
  307.8 5.6 pad_maximum_fusion
  313.4 3.9 fusion.10
  317.2 17.9 %convolution_convert_fusion.q_ref.k_ref.v_ref = bf16[2048,1536]{1,0:T(8,128)(2,1)S(1)} fusion(bf16[2048,2048]{1,0:T(8,128)(2,1)} %copy-done.5, bf16[112,2048]{1,0:T(8,128)(2,1)S(1)} %slice.62, bf16[80,2048]{1,0:T(8,128)(2,1)S(1)} %slice.61, bf16[1344,2048]{1,0:T(8,128)(2,1)} %bitcast.20), kind=kOutput, calls=%fused_computation | convolution fusion | flops 12906921984 | bytes 20971520 | tf_op jit(solution)/shard_map/dot_general | solution.py:615
  335.1 30.9 %mqa_a.1 = (bf16[2048,1024]{1,0:T(8,128)(2,1)S(1)}, bf16[2048,256]{1,0:T(8,128)(2,1)}, bf16[2048,256]{1,0:T(8,128)(2,1)}) custom-call(bf16[2048,1536]{1,0:T(8,128)(2,1)S(1)} %convolution_convert_fusion.q_ref.k_ref.v_ref, bf16[2048,1536]{1,0:T(8,128)(2,1)S(1)} %convolution_convert_fusion.q_ref.k_ref.v_ref, ...), custom_call_target="tpu_custom_call" | custom-call | flops 10737418240 | bytes 16777216 | tf_op jit(solution)/shard_map/mqa_a/pallas_call | solution.py:270
  366.0 0.0 copy-start.3
  366.0 2.1 copy-done.3
  368.1 39.4 %shard_map.69.refs_2_ = bf16[16576,2048]{1,0:T(8,128)(2,1)} custom-call(bf16[4096,2048]{1,0:T(8,128)(2,1)} %get-tuple-element.17.refs_0_, bf16[2048,2048]{1,0:T(8,128)(2,1)} %get-tuple-element.13.refs_1_, bf16[16576,2048]{1,0:T(8,128)(2,1)} %get-tuple-element.18.refs_2_), custom_call_target="tpu_custom_call", output_to_operand_aliasing={{}: (2, {})} | custom-call | flops 30064771072 | bytes 29360128 | tf_op jit(solution)/shard_map/pallas_call | solution.py:382
  407.5 0.0 copy-start.1
  407.5 0.0 all-gather.4.cloned.1.call-done.refs_0_
  407.6 0.0 copy-start.2
  407.6 12.7 %fusion.7.q_ref = bf16[2048,1024]{1,0:T(8,128)(2,1)S(1)} fusion(bf16[2048,2048]{1,0:T(8,128)(2,1)} %copy-done.5, bf16[8192,2048]{1,0:T(8,128)(2,1)} %all-gather.4.cloned.1.call-done.refs_0_), kind=kOutput, calls=%fused_computation.9 | convolution fusion | flops 8592031744 | bytes 16777216 | tf_op jit(solution)/shard_map/dot_general | solution.py:615
  420.3 0.0 copy-done.1
  420.3 0.0 copy-done.2
  420.3 30.3 %mqa_b.1.refs_5_ = bf16[2048,1024]{1,0:T(8,128)(2,1)S(1)} custom-call(bf16[2048,1024]{1,0:T(8,128)(2,1)S(1)} %fusion.7.q_ref, bf16[2048,256]{1,0:T(8,128)(2,1)S(1)} %copy-done.1, bf16[2048,256]{1,0:T(8,128)(2,1)S(1)} %copy-done.2, f32[2048,128]{1,0:T(8,128)S(1)} %get-tuple-element.26.cos_ref, f32[2048,128]{1,0:T(8,128)S(1)} %get-tuple-element.25.sin_ref), custom_call_target="tpu_custom_call" | custom-call | flops 10737418240 | bytes 16777216 | tf_op jit(solution)/shard_map/mqa_b/pallas_call | solution.py:270
  450.6 0.0 copy-start.4
  450.6 1.9 copy-done.4
  452.5 70.8 %shard_map.70.refs_0_ = bf16[16576,2048]{1,0:T(8,128)(2,1)} custom-call(bf16[8192,2048]{1,0:T(8,128)(2,1)} %all-gather.4.cloned.1.call-done.refs_0_, bf16[2048,2048]{1,0:T(8,128)(2,1)} %get-tuple-element.13.refs_1_, bf16[16576,2048]{1,0:T(8,128)(2,1)} %shard_map.69.refs_2_), custom_call_target="tpu_custom_call", output_to_operand_aliasing={{}: (2, {})} | custom-call | flops 60129542144 | bytes 58720256 | tf_op jit(solution)/shard_map/pallas_call | solution.py:382
  523.4 0.0 all-gather.8.cloned.1.call-done.refs_1_.refs_3_
  523.4 56.8 %out_proj_a.1.refs_2_ = f32[2048,2048]{1,0:T(8,128)} custom-call(bf16[16576,2048]{1,0:T(8,128)(2,1)} %shard_map.70.refs_0_, bf16[6144,2048]{1,0:T(8,128)(2,1)} %all-gather.8.cloned.1.call-done.refs_1_.refs_3_), custom_call_target="tpu_custom_call" | custom-call | flops 40802189312 | bytes 59768832 | tf_op jit(solution)/shard_map/out_proj_a/pallas_call | solution.py:559
  580.2 0.0 all-gather.6.cloned.1.call-done.refs_1_
  580.3 61.1 %out_proj_b.1 = bf16[2048,2048]{1,0:T(8,128)(2,1)} custom-call(bf16[16576,2048]{1,0:T(8,128)(2,1)} %shard_map.70.refs_0_, bf16[4096,2048]{1,0:T(8,128)(2,1)} %all-gather.6.cloned.1.call-done.refs_1_, f32[2048,2048]{1,0:T(8,128)} %out_proj_a.1.refs_2_, bf16[6144,2048]{1,0:T(8,128)(2,1)} %all-gather.8.cloned.1.call-done.refs_1_.refs_3_, ...), custom_call_target="tpu_custom_call" | custom-call | flops 45097156608 | bytes 66060288 | tf_op jit(solution)/shard_map/out_proj_b/pallas_call | solution.py:559
  (3 shorter events, 0.0 us)
Async XLA Ops:
  7.2 6.9 %copy-start.6 = (bf16[2048,592]{0,1:T(8,128)(2,1)S(1)}, bf16[2048,592]{0,1:T(8,128)(2,1)}, u32[]{:S(2)}) copy-start(bf16[2048,592]{0,1:T(8,128)(2,1)} %param.6) | copy-start | bytes 7274500
  7.2 7.2 %copy-start = (f32[2048]{0:T(1024)S(1)}, f32[2048]{0:T(1024)}, u32[]{:S(2)}) copy-start(f32[2048]{0:T(1024)} %param.5) | copy-start | bytes 24580
  7.2 400.3 %all-gather.4.cloned.1.call-start = ((), (), s32[]{:S(2)}) async-start(), calls=%async_computation | async-start | bytes 34603008 | tf_op jit(solution)/shard_map/all_gather | solution.py:582
  9.8 513.5 %all-gather.8.cloned.1.call-start = ((), (), s32[]{:S(2)}) async-start(), calls=%async_computation.2 | async-start | bytes 25952256 | tf_op jit(solution)/shard_map/all_gather | solution.py:582
  12.1 568.2 %all-gather.6.cloned.1.call-start = ((), (), s32[]{:S(2)}) async-start(), calls=%async_computation.1 | async-start | bytes 17301504 | tf_op jit(solution)/shard_map/all_gather | solution.py:582
  96.6 3.4 copy-start.5
  366.0 2.1 copy-start.3
  407.5 12.7 %copy-start.1 = (bf16[2048,256]{1,0:T(8,128)(2,1)S(1)}, bf16[2048,256]{1,0:T(8,128)(2,1)}, u32[]{:S(2)}) copy-start(bf16[2048,256]{1,0:T(8,128)(2,1)} %get-tuple-element.21.k_ref) | copy-start | bytes 3145732
  407.6 12.7 %copy-start.2 = (bf16[2048,256]{1,0:T(8,128)(2,1)S(1)}, bf16[2048,256]{1,0:T(8,128)(2,1)}, u32[]{:S(2)}) copy-start(bf16[2048,256]{1,0:T(8,128)(2,1)} %get-tuple-element.22.v_ref) | copy-start | bytes 3145732
  450.6 1.9 copy-start.4
Sparse Core Ops, SparseCore 0:
  10.1 144.3 all-gather.3
  156.7 110.1 all-gather.7
  269.0 69.8 all-gather.5
